TPU v7x, 32 devices: a whole 2x2x4 slice. The times are simulated.
32 devices in a mesh: groups: 2 (over y), vocab: 16 (over z, x, core).
Axes of the slice: x: 2, y: 2, z: 4, core: 2. Of those that a mesh axis runs over, the one named last changes fastest.
Arguments:
- hidden: bfloat16 [512, 1280], P(('groups', 'vocab')), parts along dimension 0, may hold values from -320 to 320
- embedding: bfloat16 [6144, 1280], P('vocab'), may hold values from -0.15625 to 0.15625
- prev_tokens: int32 [2, 512], P(None, 'groups'), parts along dimension 1, may hold values from 0 to 6143, as said below
- last_stamp: int32 [512], P('groups'), parts along dimension 0, may hold values from -1 to 1500, as said below
- sample_begin: int32 [512], P('groups'), parts along dimension 0, may hold values from 1 to 4
- seq_length: int32 [512], P('groups'), parts along dimension 0, may hold values from 1 to 9, as said below
- chosen: int32 [5, 512], P(None, 'groups'), parts along dimension 1, may hold values from 0 to 6143
Outputs:
- picked_logprob: float32 [5, 512], P(None, ('groups', 'vocab')), parts along dimension 1
- stamp_logprob: float32 [512], P(('groups', 'vocab')), parts along dimension 0
There are 2 independent parts, one for each index of `groups`. A program takes and returns all parts, laid end to end along the dimension named above; an argument that names none is the same for every part. Nothing has to cross between parts.
Inputs may be any that keep to these rules, and one draw needn't show every extreme that they name: prev_tokens[1, r] is row r's latest token and prev_tokens[0, r] the one before; ids at or above 4643 are timestamps. `last_stamp`: index among the 1501 timestamps of the latest timestamp token sampled since the row's sample begin, -1 if none; equal to the latest token's index when that token is a timestamp and was sampled. `seq_length`: at least the row's sample_begin and at most sample_begin + 5.
All inputs are finite; a program needn't handle non-finite values.
Results may differ from a plain program's by a relative error of at most 0.0003.
Values may be sent and summed in bfloat16 or wider, within the bound.
No kernel may reach another device: no remote copies, remote signals or barrier semaphores. Data moves between devices by JAX's collectives and lax.ppermute only.
A program may use at most 64 MiB of HBM per device.

v0:
```python
import functools

import jax
import jax.numpy as jnp
from jax import lax
from jax.experimental import pallas as pl
from jax.experimental.pallas import tpu as pltpu
from jax.sharding import PartitionSpec as P

TSN = 1501
SPECIALS = 108
INITIAL = 50

MASK_VALUE = -1000000000.0
EMPTY_VALUE = -3000000000.0
SLOPE = 4.0
FLOOR = -30.0


LANES = 128
FIELDS = 8
FAR = 1 << 30
GRANT = 24 << 20
NEAR = 4

DIRECT = (1,)


def source_of(piece, member, outer):
    if outer > NEAR:
        return piece
    step, side = piece % outer, piece // outer
    place = lax.rem(lax.div(member, 2) + step, outer)
    return 2 * place + (lax.rem(member, 2) ^ side)


def row_limits(prev_old, prev_new, last_stamp, sample_begin, seq_length, stamp_begin):
    generated = seq_length - sample_begin
    last_is = (generated >= 1) & (prev_new >= stamp_begin)
    before_is = (generated < 2) | (prev_old >= stamp_begin)
    both = last_is & before_is
    single = last_is & ~before_is
    begin = generated == 0
    text_low = jnp.where(begin, stamp_begin, jnp.where(single, stamp_begin - SPECIALS, 0))
    bound = stamp_begin + last_stamp + jnp.where(single, 0, 1)
    stamp_low = jnp.where(both, FAR, jnp.where(last_stamp >= 0, bound, stamp_begin))
    stamp_high = jnp.where(begin, stamp_begin + INITIAL + 1, FAR)
    return text_low, stamp_low, stamp_high


def prep_kernel(members, row_dev, stamp_begin, *refs):
    prev_in, stamp_in, begin_in, length_in, chosen_in, table, own = refs[:7]
    out, table_out, own_out = refs[7:10]
    prev, stamp, begin, length, chosen, sems = refs[10:]
    copies = [
        pltpu.make_async_copy(source, target, sems.at[i])
        for i, (source, target) in enumerate((
            (prev_in, prev), (stamp_in, stamp), (begin_in, begin), (length_in, length),
            (chosen_in, chosen), (own, own_out), (table, table_out),
        ))
    ]
    for copy in copies:
        copy.start()
    for copy in copies[:5]:
        copy.wait()
    index = lax.axis_index("vocab")
    per_tile = LANES // row_dev
    lane = lax.broadcasted_iota(jnp.int32, (FIELDS, LANES), 1)
    for tile in range(members // per_tile):
        total = jnp.zeros((FIELDS, LANES), jnp.int32)
        for place in range(per_tile):
            owner = source_of(tile * per_tile + place, lax.div(index, 2), members // 2)
            source = 2 * owner + lax.rem(index, 2)
            at = pl.multiple_of(lax.div(source, per_tile) * LANES, LANES)
            span = pl.ds(at, LANES)
            limits = row_limits(
                prev[0:1, span], prev[1:2, span], stamp[:, span], begin[:, span], length[:, span],
                stamp_begin,
            )
            fields = jnp.concatenate(list(limits) + [chosen[:, span]], axis=0)
            shift = lax.rem(place - lax.rem(source, per_tile) + per_tile, per_tile) * row_dev
            moved = pltpu.roll(fields, shift, 1)
            here = (lane >= place * row_dev) & (lane < (place + 1) * row_dev)
            total = jnp.where(here, moved, total)
        out[:, tile * LANES:(tile + 1) * LANES] = total
    for copy in copies[5:]:
        copy.wait()


def stats_kernel(members, row_dev, stamp_begin, *refs):
    *parts, table, other, limits, out = refs
    index = lax.axis_index("vocab")
    member = lax.div(index, 2)
    outer = members // 2
    width = table.shape[0]
    per_tile = LANES // row_dev
    if outer > NEAR:
        pieces = parts[0][...]
    else:
        pieces = jnp.concatenate([part[...] for part in parts], axis=0)
    for tile in range(members // per_tile):
        span = slice(tile * LANES, (tile + 1) * LANES)
        rows = pieces[span]
        lim = limits[:, span]
        text_low, stamp_low, stamp_high = lim[0:1], lim[1:2], lim[2:3]
        halves = []
        for ref, shard in ((table, index), (other, index ^ 1)):
            logits = lax.dot_general(
                ref[...], rows, (((1,), (1,)), ((), ())), preferred_element_type=jnp.float32
            )
            column = shard * width + lax.broadcasted_iota(jnp.int32, (width, LANES), 0)
            is_text = column < stamp_begin
            low = jnp.where(is_text, text_low, stamp_low)
            high = jnp.where(is_text, stamp_begin - 1, stamp_high)
            values = jnp.where((column >= low) & (column < high), logits, MASK_VALUE)
            halves.append((values, column, is_text))
        text_max = stamp_max = None
        for values, column, is_text in halves:
            text = jnp.max(jnp.where(is_text, values, EMPTY_VALUE), axis=0, keepdims=True)
            stamp = jnp.max(jnp.where(is_text, EMPTY_VALUE, values), axis=0, keepdims=True)
            text_max = text if text_max is None else jnp.maximum(text_max, text)
            stamp_max = stamp if stamp_max is None else jnp.maximum(stamp_max, stamp)
        text_total = jnp.zeros((1, LANES), jnp.float32)
        stamp_total = jnp.zeros((1, LANES), jnp.float32)
        picked = [jnp.zeros((1, LANES), jnp.float32) for _ in range(FIELDS - 3)]
        for values, column, is_text in halves:
            scaled = jnp.exp(values - jnp.where(is_text, text_max, stamp_max))
            text_total += jnp.sum(jnp.where(is_text, scaled, 0.0), axis=0, keepdims=True)
            stamp_total += jnp.sum(jnp.where(is_text, 0.0, scaled), axis=0, keepdims=True)
            for k in range(FIELDS - 3):
                hit = column == lim[3 + k:4 + k]
                picked[k] += jnp.sum(jnp.where(hit, values, 0.0), axis=0, keepdims=True)
        stats = [text_max, text_max + jnp.log(text_total), stamp_max + jnp.log(stamp_total)] + picked
        lane = lax.broadcasted_iota(jnp.int32, (per_tile, LANES), 1)
        packed = jnp.zeros((per_tile, LANES), jnp.float32)
        stacked = jnp.concatenate([stats[(-f) % FIELDS] for f in range(FIELDS)], axis=0)
        turned = pltpu.roll(stacked, 0, 1, stride=row_dev, stride_axis=0)
        for f in range(FIELDS):
            spread = jnp.broadcast_to(turned[f:f + 1], (per_tile, LANES))
            moved = pltpu.roll(spread, 0, 1, stride=row_dev, stride_axis=0)
            here = (lane >= f * row_dev) & (lane < (f + 1) * row_dev)
            packed = jnp.where(here, moved, packed)
        for place in range(per_tile):
            piece = tile * per_tile + (-place) % per_tile
            target = source_of(piece, member, members // 2)
            out[pl.ds(target, 1)] = packed[place:place + 1].reshape(1, 1, LANES)


def final_kernel(row_dev, stamp_begin, got, limits, picked_out, stamp_out):
    parts = got[:, 0, :]
    top = jnp.max(parts, axis=0, keepdims=True)
    lse = top + jnp.log(jnp.sum(jnp.exp(parts - top), axis=0, keepdims=True))
    total = jnp.sum(parts, axis=0, keepdims=True)
    lane = lax.broadcasted_iota(jnp.int32, (1, LANES), 1)
    lses = lane >= (FIELDS - 2) * row_dev
    merged = jnp.where(lane < row_dev, top, jnp.where(lses, lse, total))
    spread = jnp.broadcast_to(merged, (FIELDS, LANES))
    fields = pltpu.roll(spread, 0, 1, stride=row_dev, stride_axis=0)
    text_max, text_lse, stamp_lse = fields[0:1], fields[1:2], fields[2:3]
    penalty = SLOPE * jnp.maximum(stamp_lse - text_max, 0.0)
    shifted = text_lse - penalty
    larger = jnp.maximum(shifted, stamp_lse)
    total = larger + jnp.log(jnp.exp(shifted - larger) + jnp.exp(stamp_lse - larger))
    chosen = limits[:, 0:LANES]
    adjusted = fields - jnp.where(chosen < stamp_begin, penalty, 0.0) - total
    result = jnp.maximum(adjusted, FLOOR)
    picked_out[...] = result[3:, :row_dev]
    stamp_out[...] = jnp.maximum(stamp_lse - total, FLOOR)[:, :row_dev]


def per_device(hidden, embedding, prev_tokens, last_stamp, sample_begin, seq_length, chosen):
    width = embedding.shape[0]
    row_dev = hidden.shape[0]
    nsel = chosen.shape[0]
    count = lax.axis_size("vocab")
    members = count // 2
    outer = members // 2
    stamp_begin = width * count - TSN
    core_rows = members * row_dev

    def move(array, step, side):
        pairs = [(i, ((i - 4 * step) % count) ^ (2 * side)) for i in range(count)]
        return lax.ppermute(array, "vocab", pairs)

    if outer > NEAR:
        same = [[2 * i + core for i in range(members)] for core in range(2)]
        parts = [lax.all_gather(hidden, "vocab", axis_index_groups=same, tiled=True)]
    else:
        line, across = [hidden], [move(hidden, 0, 1)]
        for step in range(1, outer):
            line.append(move(hidden, step, 0))
            origin = (hidden, step) if step in DIRECT else (line[-1], 0)
            across.append(move(*origin, 1))
        parts = line + across
    other = lax.ppermute(embedding, "vocab", [(i, i ^ 1) for i in range(count)])
    state = (prev_tokens, last_stamp[None], sample_begin[None], seq_length[None], chosen)
    limits, table, own = pl.pallas_call(
        functools.partial(prep_kernel, members, row_dev, stamp_begin),
        in_specs=[pl.BlockSpec(memory_space=pltpu.HBM)] * 7,
        out_specs=[pl.BlockSpec(memory_space=pltpu.VMEM)] * 3,
        out_shape=(
            jax.ShapeDtypeStruct((FIELDS, core_rows), jnp.int32),
            jax.ShapeDtypeStruct(embedding.shape, embedding.dtype),
            jax.ShapeDtypeStruct(hidden.shape, hidden.dtype),
        ),
        scratch_shapes=[pltpu.VMEM(part.shape, part.dtype) for part in state]
        + [pltpu.SemaphoreType.DMA((7,))],
        name="prep",
        compiler_params=pltpu.CompilerParams(vmem_limit_bytes=GRANT),
    )(*(pltpu.with_memory_space_constraint(part, pltpu.HBM) for part in (*state, embedding, hidden)))
    if outer <= NEAR:
        parts[0] = own
    stats = pl.pallas_call(
        functools.partial(stats_kernel, members, row_dev, stamp_begin),
        out_shape=jax.ShapeDtypeStruct((members, 1, LANES), jnp.float32),
        name="stats",
        compiler_params=pltpu.CompilerParams(vmem_limit_bytes=GRANT),
    )(*parts, table, other, limits)
    same_core = [[2 * i + core for i in range(members)] for core in range(2)]
    got = lax.all_to_all(stats, "vocab", 0, 0, axis_index_groups=same_core, tiled=True)
    picked, stamped = pl.pallas_call(
        functools.partial(final_kernel, row_dev, stamp_begin),
        out_shape=(
            jax.ShapeDtypeStruct((nsel, row_dev), jnp.float32),
            jax.ShapeDtypeStruct((1, row_dev), jnp.float32),
        ),
        name="final",
        compiler_params=pltpu.CompilerParams(vmem_limit_bytes=GRANT),
    )(got, limits)
    return picked, stamped[0]


def solution(mesh):
    placed = (
        P(("groups", "vocab"), None),
        P("vocab", None),
        P(None, "groups"),
        P("groups"),
        P("groups"),
        P("groups"),
        P(None, "groups"),
    )
    return jax.shard_map(
        per_device,
        mesh=mesh,
        in_specs=placed,
        out_specs=(P(None, ("groups", "vocab")), P(("groups", "vocab"))),
        check_vma=False,
    )
```

profile of v0, /device:TPU:0, one launch (start us, length us, event | category | flops | bytes accessed | tf_op | source)
XLA Modules:
  0.0 28.2 jit_solution(9071715837673068708)
XLA Ops:
  0.6 0.6 %collective-permute-start.7 = (bf16[384,1280]{1,0:T(8,128)(2,1)}, bf16[384,1280]{1,0:T(8,128)(2,1)S(1)}, u32[]{:S(2)}, u32[]{:S(2)}) collective-permute-start(bf16[384,1280]{1,0:T(8,128)(2,1)} %refs_5_.1), channel_id=1, source_target_pairs={{0,1},{1,0},{2,3},{3,2},{4,5},{5,4},{6,7},{7,6},{8,9},{9,8},{10,11... | collective-permute-start | bytes 2949128 | tf_op jit(solution)/shard_map/ppermute | solution.py:195
  1.2 2.6 %collective-permute-start.2 = (bf16[16,1280]{1,0:T(8,128)(2,1)}, bf16[16,1280]{1,0:T(8,128)(2,1)S(1)}, u32[]{:S(2)}, u32[]{:S(2)}) collective-permute-start(bf16[16,1280]{1,0:T(8,128)(2,1)} %refs_6_.1), channel_id=1, source_target_pairs={{0,4},{1,5},{2,6},{3,7},{4,8},{5,9},{6,10},{7,11},{8,12},{9,13},{1... | collective-permute-start | bytes 122888 | tf_op jit(solution)/shard_map/ppermute | solution.py:183
  3.8 2.6 %collective-permute-start.1 = (bf16[16,1280]{1,0:T(8,128)(2,1)}, bf16[16,1280]{1,0:T(8,128)(2,1)S(1)}, u32[]{:S(2)}, u32[]{:S(2)}) collective-permute-start(bf16[16,1280]{1,0:T(8,128)(2,1)} %refs_6_.1), channel_id=1, source_target_pairs={{0,8},{1,9},{2,10},{3,11},{4,12},{5,13},{6,14},{7,15},{8,0},{9,1},... | collective-permute-start | bytes 122888 | tf_op jit(solution)/shard_map/ppermute | solution.py:183
  6.4 1.3 %collective-permute-start = (bf16[16,1280]{1,0:T(8,128)(2,1)}, bf16[16,1280]{1,0:T(8,128)(2,1)S(1)}, u32[]{:S(2)}, u32[]{:S(2)}) collective-permute-start(bf16[16,1280]{1,0:T(8,128)(2,1)} %refs_6_.1), channel_id=1, source_target_pairs={{0,12},{1,13},{2,14},{3,15},{4,0},{5,1},{6,2},{7,3},{8,4},{9,5},{1... | collective-permute-start | bytes 122888 | tf_op jit(solution)/shard_map/ppermute | solution.py:183
  7.8 1.4 %collective-permute-start.4 = (bf16[16,1280]{1,0:T(8,128)(2,1)}, bf16[16,1280]{1,0:T(8,128)(2,1)S(1)}, u32[]{:S(2)}, u32[]{:S(2)}) collective-permute-start(bf16[16,1280]{1,0:T(8,128)(2,1)} %refs_6_.1), channel_id=1, source_target_pairs={{0,14},{1,15},{2,12},{3,13},{4,2},{5,3},{6,0},{7,1},{8,6},{9,7},{1... | collective-permute-start | bytes 122888 | tf_op jit(solution)/shard_map/ppermute | solution.py:183
  9.1 0.0 collective-permute-done.2.refs_3_
  9.1 0.7 %collective-permute-start.3 = (bf16[16,1280]{1,0:T(8,128)(2,1)}, bf16[16,1280]{1,0:T(8,128)(2,1)S(1)}, u32[]{:S(2)}, u32[]{:S(2)}) collective-permute-start(bf16[16,1280]{1,0:T(8,128)(2,1)} %refs_6_.1), channel_id=1, source_target_pairs={{0,2},{1,3},{2,0},{3,1},{4,6},{5,7},{6,4},{7,5},{8,10},{9,11},{10,... | collective-permute-start | bytes 122888 | tf_op jit(solution)/shard_map/ppermute | solution.py:183
  9.8 0.5 %collective-permute-done.1.refs_2_ = bf16[16,1280]{1,0:T(8,128)(2,1)S(1)} collective-permute-done((bf16[16,1280]{1,0:T(8,128)(2,1)}, bf16[16,1280]{1,0:T(8,128)(2,1)S(1)}, u32[]{:S(2)}, u32[]{:S(2)}) %collective-permute-start.1) | collective-permute-done | bytes 40992 | tf_op jit(solution)/shard_map/ppermute | solution.py:183
  10.2 1.5 %collective-permute-start.6 = (bf16[16,1280]{1,0:T(8,128)(2,1)S(1)}, bf16[16,1280]{1,0:T(8,128)(2,1)S(1)}, u32[]{:S(2)}, u32[]{:S(2)}) collective-permute-start(bf16[16,1280]{1,0:T(8,128)(2,1)S(1)} %collective-permute-done.2.refs_3_), channel_id=1, source_target_pairs={{0,2},{1,3},{2,0},{3,1},{4,6},{5,7},{6,4},{7,5},{8,10},{9,11},{10,... | collective-permute-start | bytes 122888 | tf_op jit(solution)/shard_map/ppermute | solution.py:183
  11.7 0.0 collective-permute-done.refs_1_
  11.7 0.8 %collective-permute-start.5 = (bf16[16,1280]{1,0:T(8,128)(2,1)S(1)}, bf16[16,1280]{1,0:T(8,128)(2,1)S(1)}, u32[]{:S(2)}, u32[]{:S(2)}) collective-permute-start(bf16[16,1280]{1,0:T(8,128)(2,1)S(1)} %collective-permute-done.1.refs_2_), channel_id=1, source_target_pairs={{0,2},{1,3},{2,0},{3,1},{4,6},{5,7},{6,4},{7,5},{8,10},{9,11},{10,... | collective-permute-start | bytes 122888 | tf_op jit(solution)/shard_map/ppermute | solution.py:183
  12.6 1.4 %prep.1 = (s32[8,128]{1,0:T(8,128)S(1)}, bf16[384,1280]{1,0:T(8,128)(2,1)S(1)}, bf16[16,1280]{1,0:T(8,128)(2,1)S(1)}) custom-call(s32[2,256]{1,0:T(2,128)} %refs_0_.1, s32[1,256]{1,0:T(1,128)} %bitcast.4, s32[1,256]{1,0:T(1,128)} %bitcast.5, s32[1,256]{1,0:T(1,128)} %bitcast.6, s32[5,256]{1,0:T(8,128)} %refs_4_.1, bf16[384,1280]{1,0:T(8,128)(2,1)} %refs_5_.1, ...), custom_call_target="tpu_custom_call" | custom-call | tf_op jit(solution)/shard_map/prep/pallas_call | solution.py:197
  13.9 0.0 collective-permute-done.4.refs_5_
  13.9 0.0 collective-permute-done.3.refs_4_
  14.0 0.3 %collective-permute-done.6.refs_7_ = bf16[16,1280]{1,0:T(8,128)(2,1)S(1)} collective-permute-done((bf16[16,1280]{1,0:T(8,128)(2,1)S(1)}, bf16[16,1280]{1,0:T(8,128)(2,1)S(1)}, u32[]{:S(2)}, u32[]{:S(2)}) %collective-permute-start.6) | collective-permute-done | bytes 40992 | tf_op jit(solution)/shard_map/ppermute | solution.py:183
  14.2 1.5 %collective-permute-done.5.refs_6_ = bf16[16,1280]{1,0:T(8,128)(2,1)S(1)} collective-permute-done((bf16[16,1280]{1,0:T(8,128)(2,1)S(1)}, bf16[16,1280]{1,0:T(8,128)(2,1)S(1)}, u32[]{:S(2)}, u32[]{:S(2)}) %collective-permute-start.5) | collective-permute-done | bytes 40992 | tf_op jit(solution)/shard_map/ppermute | solution.py:183
  15.7 0.0 collective-permute-done.7.refs_9_
  15.7 1.2 %stats.1 = f32[8,1,128]{2,1,0:T(1,128)S(1)} custom-call(bf16[16,1280]{1,0:T(8,128)(2,1)S(1)} %get-tuple-element.7.refs_0_, bf16[16,1280]{1,0:T(8,128)(2,1)S(1)} %collective-permute-done.refs_1_, bf16[16,1280]{1,0:T(8,128)(2,1)S(1)} %collective-permute-done.1.refs_2_, bf16[16,1280]{1,0:T(8,128)(2,1)S(1)} %collective-permute-done.2.refs_3_, ...), custom_call_target="tpu_custom_call" | custom-call | tf_op jit(solution)/shard_map/stats/pallas_call | solution.py:213
  17.0 10.5 %all_to_all.5.got = f32[8,1,128]{2,1,0:T(1,128)S(1)} all-to-all(f32[8,1,128]{2,1,0:T(1,128)S(1)} %stats.1), channel_id=1, replica_groups={{0,2,4,6,8,10,12,14},{1,3,5,7,9,11,13,15},{16,18,20,22,24,26,28,30},{17..., dimensions={0} | all-to-all | bytes 8192 | tf_op jit(solution)/shard_map/all_to_all | solution.py:220
  27.5 0.7 %final.1 = (f32[5,16]{1,0:T(8,128)}, f32[1,16]{1,0:T(1,128)}) custom-call(f32[8,1,128]{2,1,0:T(1,128)S(1)} %all_to_all.5.got, s32[8,128]{1,0:T(8,128)S(1)} %get-tuple-element.9.refs_10_.limits), custom_call_target="tpu_custom_call" | custom-call | tf_op jit(solution)/shard_map/final/pallas_call | solution.py:221
Async XLA Ops:
  0.6 15.1 %collective-permute-start.7 = (bf16[384,1280]{1,0:T(8,128)(2,1)}, bf16[384,1280]{1,0:T(8,128)(2,1)S(1)}, u32[]{:S(2)}, u32[]{:S(2)}) collective-permute-start(bf16[384,1280]{1,0:T(8,128)(2,1)} %refs_5_.1), channel_id=1, source_target_pairs={{0,1},{1,0},{2,3},{3,2},{4,5},{5,4},{6,7},{7,6},{8,9},{9,8},{10,11... | collective-permute-start | bytes 2949128 | tf_op jit(solution)/shard_map/ppermute | solution.py:195
  1.2 7.9 %collective-permute-start.2 = (bf16[16,1280]{1,0:T(8,128)(2,1)}, bf16[16,1280]{1,0:T(8,128)(2,1)S(1)}, u32[]{:S(2)}, u32[]{:S(2)}) collective-permute-start(bf16[16,1280]{1,0:T(8,128)(2,1)} %refs_6_.1), channel_id=1, source_target_pairs={{0,4},{1,5},{2,6},{3,7},{4,8},{5,9},{6,10},{7,11},{8,12},{9,13},{1... | collective-permute-start | bytes 122888 | tf_op jit(solution)/shard_map/ppermute | solution.py:183
  3.8 6.4 %collective-permute-start.1 = (bf16[16,1280]{1,0:T(8,128)(2,1)}, bf16[16,1280]{1,0:T(8,128)(2,1)S(1)}, u32[]{:S(2)}, u32[]{:S(2)}) collective-permute-start(bf16[16,1280]{1,0:T(8,128)(2,1)} %refs_6_.1), channel_id=1, source_target_pairs={{0,8},{1,9},{2,10},{3,11},{4,12},{5,13},{6,14},{7,15},{8,0},{9,1},... | collective-permute-start | bytes 122888 | tf_op jit(solution)/shard_map/ppermute | solution.py:183
  6.4 5.3 %collective-permute-start = (bf16[16,1280]{1,0:T(8,128)(2,1)}, bf16[16,1280]{1,0:T(8,128)(2,1)S(1)}, u32[]{:S(2)}, u32[]{:S(2)}) collective-permute-start(bf16[16,1280]{1,0:T(8,128)(2,1)} %refs_6_.1), channel_id=1, source_target_pairs={{0,12},{1,13},{2,14},{3,15},{4,0},{5,1},{6,2},{7,3},{8,4},{9,5},{1... | collective-permute-start | bytes 122888 | tf_op jit(solution)/shard_map/ppermute | solution.py:183
  7.8 6.2 %collective-permute-start.4 = (bf16[16,1280]{1,0:T(8,128)(2,1)}, bf16[16,1280]{1,0:T(8,128)(2,1)S(1)}, u32[]{:S(2)}, u32[]{:S(2)}) collective-permute-start(bf16[16,1280]{1,0:T(8,128)(2,1)} %refs_6_.1), channel_id=1, source_target_pairs={{0,14},{1,15},{2,12},{3,13},{4,2},{5,3},{6,0},{7,1},{8,6},{9,7},{1... | collective-permute-start | bytes 122888 | tf_op jit(solution)/shard_map/ppermute | solution.py:183
  9.1 4.8 %collective-permute-start.3 = (bf16[16,1280]{1,0:T(8,128)(2,1)}, bf16[16,1280]{1,0:T(8,128)(2,1)S(1)}, u32[]{:S(2)}, u32[]{:S(2)}) collective-permute-start(bf16[16,1280]{1,0:T(8,128)(2,1)} %refs_6_.1), channel_id=1, source_target_pairs={{0,2},{1,3},{2,0},{3,1},{4,6},{5,7},{6,4},{7,5},{8,10},{9,11},{10,... | collective-permute-start | bytes 122888 | tf_op jit(solution)/shard_map/ppermute | solution.py:183
  10.2 4.0 %collective-permute-start.6 = (bf16[16,1280]{1,0:T(8,128)(2,1)S(1)}, bf16[16,1280]{1,0:T(8,128)(2,1)S(1)}, u32[]{:S(2)}, u32[]{:S(2)}) collective-permute-start(bf16[16,1280]{1,0:T(8,128)(2,1)S(1)} %collective-permute-done.2.refs_3_), channel_id=1, source_target_pairs={{0,2},{1,3},{2,0},{3,1},{4,6},{5,7},{6,4},{7,5},{8,10},{9,11},{10,... | collective-permute-start | bytes 122888 | tf_op jit(solution)/shard_map/ppermute | solution.py:183
  11.7 4.0 %collective-permute-start.5 = (bf16[16,1280]{1,0:T(8,128)(2,1)S(1)}, bf16[16,1280]{1,0:T(8,128)(2,1)S(1)}, u32[]{:S(2)}, u32[]{:S(2)}) collective-permute-start(bf16[16,1280]{1,0:T(8,128)(2,1)S(1)} %collective-permute-done.1.refs_2_), channel_id=1, source_target_pairs={{0,2},{1,3},{2,0},{3,1},{4,6},{5,7},{6,4},{7,5},{8,10},{9,11},{10,... | collective-permute-start | bytes 122888 | tf_op jit(solution)/shard_map/ppermute | solution.py:183
where the time goes:
time: 28.4 us; the launch traced here: 28.2 us
  starting transfers between devices  11.5 us (40%)
  blocking collectives  10.5 us (37%)
  Pallas kernels  3.33 us (12%)
  waiting for transfers between devices  2.26 us (8%)
  between operations  0.67 us (2%)
    ppermute x7, starting transfers between devices, move(): return lax.ppermute(array, 'vocab', pairs)  10.9 us
    all_to_all x1, blocking collectives, per_device(): lax.all_to_all(stats, 'vocab', 0, 0, axis_index_groups=same_core, tiled=T...  10.5 us
    ppermute x7, waiting for transfers between devices, move(): return lax.ppermute(array, 'vocab', pairs)  2.26 us
    pallas_call x1, Pallas kernels, per_device(): pl.pallas_call(functools.partial(prep_kernel, members, row_dev, stamp_beg...  1.37 us
    pallas_call x1, Pallas kernels, per_device(): pl.pallas_call(functools.partial(stats_kernel, members, row_dev, stamp_be...  1.24 us
    pallas_call x1, Pallas kernels, per_device(): pl.pallas_call(functools.partial(final_kernel, row_dev, stamp_begin), out...  0.73 us
  transfers between devices with their start and end apart: 8, of which 3 were waited for; matrix products, arithmetic and copies ran while one was open for 0% of the time, Pallas kernels for 5%

commit v1 on v0

--- a/solution.py
+++ b/solution.py
@@ -18,6 +18,7 @@
 
 
 LANES = 128
+SUBLANES = 8
 FIELDS = 8
 FAR = 1 << 30
 GRANT = 24 << 20
@@ -94,43 +95,62 @@
     outer = members // 2
     width = table.shape[0]
     per_tile = LANES // row_dev
-    if outer > NEAR:
-        pieces = parts[0][...]
-    else:
-        pieces = jnp.concatenate([part[...] for part in parts], axis=0)
-    for tile in range(members // per_tile):
-        span = slice(tile * LANES, (tile + 1) * LANES)
-        rows = pieces[span]
-        lim = limits[:, span]
+    home, edge = divmod(stamp_begin, width)
+    edge_at = edge // SUBLANES * SUBLANES
+    block = (SUBLANES, LANES)
+    within = lax.broadcasted_iota(jnp.int32, block, 0)
+
+    def wide(row):
+        return jnp.broadcast_to(row, block)
+
+    def tile_stats(rows, lim, tile):
         text_low, stamp_low, stamp_high = lim[0:1], lim[1:2], lim[2:3]
-        halves = []
+        picked = [jnp.zeros(block, jnp.float32) for _ in range(FIELDS - 3)]
+        segments = []
         for ref, shard in ((table, index), (other, index ^ 1)):
+            base = shard * width
             logits = lax.dot_general(
                 ref[...], rows, (((1,), (1,)), ((), ())), preferred_element_type=jnp.float32
             )
-            column = shard * width + lax.broadcasted_iota(jnp.int32, (width, LANES), 0)
-            is_text = column < stamp_begin
-            low = jnp.where(is_text, text_low, stamp_low)
-            high = jnp.where(is_text, stamp_begin - 1, stamp_high)
-            values = jnp.where((column >= low) & (column < high), logits, MASK_VALUE)
-            halves.append((values, column, is_text))
-        text_max = stamp_max = None
-        for values, column, is_text in halves:
-            text = jnp.max(jnp.where(is_text, values, EMPTY_VALUE), axis=0, keepdims=True)
-            stamp = jnp.max(jnp.where(is_text, EMPTY_VALUE, values), axis=0, keepdims=True)
-            text_max = text if text_max is None else jnp.maximum(text_max, text)
-            stamp_max = stamp if stamp_max is None else jnp.maximum(stamp_max, stamp)
-        text_total = jnp.zeros((1, LANES), jnp.float32)
-        stamp_total = jnp.zeros((1, LANES), jnp.float32)
-        picked = [jnp.zeros((1, LANES), jnp.float32) for _ in range(FIELDS - 3)]
-        for values, column, is_text in halves:
-            scaled = jnp.exp(values - jnp.where(is_text, text_max, stamp_max))
-            text_total += jnp.sum(jnp.where(is_text, scaled, 0.0), axis=0, keepdims=True)
-            stamp_total += jnp.sum(jnp.where(is_text, 0.0, scaled), axis=0, keepdims=True)
-            for k in range(FIELDS - 3):
-                hit = column == lim[3 + k:4 + k]
-                picked[k] += jnp.sum(jnp.where(hit, values, 0.0), axis=0, keepdims=True)
-        stats = [text_max, text_max + jnp.log(text_total), stamp_max + jnp.log(stamp_total)] + picked
+            wanted = [wide(lim[3 + k:4 + k] - base) for k in range(FIELDS - 3)]
+            for first, last in zip((0, edge_at, edge_at + SUBLANES), (edge_at, edge_at + SUBLANES, width)):
+                if first == last:
+                    continue
+                if first == edge_at:
+                    is_text = base + first + within < stamp_begin
+                else:
+                    is_text = wide(jnp.full((1, LANES), shard) < home + (1 if first < edge_at else 0))
+                low = jnp.where(is_text, wide(text_low), wide(stamp_low)) - base
+                high = jnp.where(is_text, stamp_begin - 1, wide(stamp_high)) - base
+                values, top = [], None
+                for at in range(first, last, SUBLANES):
+                    column = within + at
+                    open_here = (column >= low) & (column < high)
+                    value = jnp.where(open_here, logits[at:at + SUBLANES], MASK_VALUE)
+                    values.append(value)
+                    top = value if top is None else jnp.maximum(top, value)
+                    for k in range(FIELDS - 3):
+                        picked[k] = jnp.where(column == wanted[k], value, picked[k])
+                segments.append((is_text, values, top))
+        text_top = stamp_top = jnp.full(block, EMPTY_VALUE)
+        for is_text, _, top in segments:
+            text_top = jnp.maximum(text_top, jnp.where(is_text, top, EMPTY_VALUE))
+            stamp_top = jnp.maximum(stamp_top, jnp.where(is_text, EMPTY_VALUE, top))
+        text_max = jnp.max(text_top, axis=0, keepdims=True)
+        stamp_max = jnp.max(stamp_top, axis=0, keepdims=True)
+        text_total = jnp.zeros(block, jnp.float32)
+        stamp_total = jnp.zeros(block, jnp.float32)
+        for is_text, values, _ in segments:
+            top = jnp.where(is_text, wide(text_max), wide(stamp_max))
+            total = jnp.zeros(block, jnp.float32)
+            for value in values:
+                total += jnp.exp(value - top)
+            text_total += jnp.where(is_text, total, 0.0)
+            stamp_total += jnp.where(is_text, 0.0, total)
+        text_total = jnp.sum(text_total, axis=0, keepdims=True)
+        stamp_total = jnp.sum(stamp_total, axis=0, keepdims=True)
+        stats = [text_max, text_max + jnp.log(text_total), stamp_max + jnp.log(stamp_total)]
+        stats += [jnp.sum(value, axis=0, keepdims=True) for value in picked]
         lane = lax.broadcasted_iota(jnp.int32, (per_tile, LANES), 1)
         packed = jnp.zeros((per_tile, LANES), jnp.float32)
         stacked = jnp.concatenate([stats[(-f) % FIELDS] for f in range(FIELDS)], axis=0)
@@ -142,8 +162,19 @@
             packed = jnp.where(here, moved, packed)
         for place in range(per_tile):
             piece = tile * per_tile + (-place) % per_tile
-            target = source_of(piece, member, members // 2)
+            target = source_of(piece, member, outer)
             out[pl.ds(target, 1)] = packed[place:place + 1].reshape(1, 1, LANES)
+
+    if outer > NEAR:
+        @pl.loop(0, members // per_tile)
+        def _(tile):
+            span = pl.ds(pl.multiple_of(tile * LANES, LANES), LANES)
+            tile_stats(parts[0][span, :], limits[:, span], tile)
+    else:
+        rows = jnp.concatenate([part[...] for part in parts], axis=0)
+        for tile in range(members // per_tile):
+            span = slice(tile * LANES, (tile + 1) * LANES)
+            tile_stats(rows[span], limits[:, span], tile)
 
 
 def final_kernel(row_dev, stamp_begin, got, limits, picked_out, stamp_out):

time: 28.4 us -> 28.4 us (level)
  no operation moved by 1% of the time
where the time goes in v1:
time: 28.4 us; the launch traced here: 28.2 us
  starting transfers between devices  11.5 us (40%)
  blocking collectives  10.5 us (37%)
  Pallas kernels  3.31 us (12%)
  waiting for transfers between devices  2.26 us (8%)
  between operations  0.67 us (2%)
    ppermute x7, starting transfers between devices, move(): return lax.ppermute(array, 'vocab', pairs)  10.9 us
    all_to_all x1, blocking collectives, per_device(): lax.all_to_all(stats, 'vocab', 0, 0, axis_index_groups=same_core, tiled=T...  10.5 us
    ppermute x7, waiting for transfers between devices, move(): return lax.ppermute(array, 'vocab', pairs)  2.26 us
    pallas_call x1, Pallas kernels, per_device(): pl.pallas_call(functools.partial(prep_kernel, members, row_dev, stamp_beg...  1.37 us
    pallas_call x1, Pallas kernels, per_device(): pl.pallas_call(functools.partial(stats_kernel, members, row_dev, stamp_be...  1.21 us
    pallas_call x1, Pallas kernels, per_device(): pl.pallas_call(functools.partial(final_kernel, row_dev, stamp_begin), out...  0.73 us
  transfers between devices with their start and end apart: 8, of which 3 were waited for; matrix products, arithmetic and copies ran while one was open for 0% of the time, Pallas kernels for 5%

profile of v1, /device:TPU:0, one launch (start us, length us, event | category | flops | bytes accessed | tf_op | source)
XLA Modules:
  0.0 28.2 jit_solution(1704011229001238154)
XLA Ops:
  0.6 0.6 %collective-permute-start.7 = (bf16[384,1280]{1,0:T(8,128)(2,1)}, bf16[384,1280]{1,0:T(8,128)(2,1)S(1)}, u32[]{:S(2)}, u32[]{:S(2)}) collective-permute-start(bf16[384,1280]{1,0:T(8,128)(2,1)} %refs_5_.1), channel_id=1, source_target_pairs={{0,1},{1,0},{2,3},{3,2},{4,5},{5,4},{6,7},{7,6},{8,9},{9,8},{10,11... | collective-permute-start | bytes 2949128 | tf_op jit(solution)/shard_map/ppermute | solution.py:226
  1.2 2.6 %collective-permute-start.2 = (bf16[16,1280]{1,0:T(8,128)(2,1)}, bf16[16,1280]{1,0:T(8,128)(2,1)S(1)}, u32[]{:S(2)}, u32[]{:S(2)}) collective-permute-start(bf16[16,1280]{1,0:T(8,128)(2,1)} %refs_6_.1), channel_id=1, source_target_pairs={{0,4},{1,5},{2,6},{3,7},{4,8},{5,9},{6,10},{7,11},{8,12},{9,13},{1... | collective-permute-start | bytes 122888 | tf_op jit(solution)/shard_map/ppermute | solution.py:214
  3.8 2.6 %collective-permute-start.1 = (bf16[16,1280]{1,0:T(8,128)(2,1)}, bf16[16,1280]{1,0:T(8,128)(2,1)S(1)}, u32[]{:S(2)}, u32[]{:S(2)}) collective-permute-start(bf16[16,1280]{1,0:T(8,128)(2,1)} %refs_6_.1), channel_id=1, source_target_pairs={{0,8},{1,9},{2,10},{3,11},{4,12},{5,13},{6,14},{7,15},{8,0},{9,1},... | collective-permute-start | bytes 122888 | tf_op jit(solution)/shard_map/ppermute | solution.py:214
  6.4 1.3 %collective-permute-start = (bf16[16,1280]{1,0:T(8,128)(2,1)}, bf16[16,1280]{1,0:T(8,128)(2,1)S(1)}, u32[]{:S(2)}, u32[]{:S(2)}) collective-permute-start(bf16[16,1280]{1,0:T(8,128)(2,1)} %refs_6_.1), channel_id=1, source_target_pairs={{0,12},{1,13},{2,14},{3,15},{4,0},{5,1},{6,2},{7,3},{8,4},{9,5},{1... | collective-permute-start | bytes 122888 | tf_op jit(solution)/shard_map/ppermute | solution.py:214
  7.8 1.4 %collective-permute-start.4 = (bf16[16,1280]{1,0:T(8,128)(2,1)}, bf16[16,1280]{1,0:T(8,128)(2,1)S(1)}, u32[]{:S(2)}, u32[]{:S(2)}) collective-permute-start(bf16[16,1280]{1,0:T(8,128)(2,1)} %refs_6_.1), channel_id=1, source_target_pairs={{0,14},{1,15},{2,12},{3,13},{4,2},{5,3},{6,0},{7,1},{8,6},{9,7},{1... | collective-permute-start | bytes 122888 | tf_op jit(solution)/shard_map/ppermute | solution.py:214
  9.1 0.0 collective-permute-done.2.refs_3_
  9.1 0.7 %collective-permute-start.3 = (bf16[16,1280]{1,0:T(8,128)(2,1)}, bf16[16,1280]{1,0:T(8,128)(2,1)S(1)}, u32[]{:S(2)}, u32[]{:S(2)}) collective-permute-start(bf16[16,1280]{1,0:T(8,128)(2,1)} %refs_6_.1), channel_id=1, source_target_pairs={{0,2},{1,3},{2,0},{3,1},{4,6},{5,7},{6,4},{7,5},{8,10},{9,11},{10,... | collective-permute-start | bytes 122888 | tf_op jit(solution)/shard_map/ppermute | solution.py:214
  9.8 0.5 %collective-permute-done.1.refs_2_ = bf16[16,1280]{1,0:T(8,128)(2,1)S(1)} collective-permute-done((bf16[16,1280]{1,0:T(8,128)(2,1)}, bf16[16,1280]{1,0:T(8,128)(2,1)S(1)}, u32[]{:S(2)}, u32[]{:S(2)}) %collective-permute-start.1) | collective-permute-done | bytes 40992 | tf_op jit(solution)/shard_map/ppermute | solution.py:214
  10.2 1.5 %collective-permute-start.6 = (bf16[16,1280]{1,0:T(8,128)(2,1)S(1)}, bf16[16,1280]{1,0:T(8,128)(2,1)S(1)}, u32[]{:S(2)}, u32[]{:S(2)}) collective-permute-start(bf16[16,1280]{1,0:T(8,128)(2,1)S(1)} %collective-permute-done.2.refs_3_), channel_id=1, source_target_pairs={{0,2},{1,3},{2,0},{3,1},{4,6},{5,7},{6,4},{7,5},{8,10},{9,11},{10,... | collective-permute-start | bytes 122888 | tf_op jit(solution)/shard_map/ppermute | solution.py:214
  11.7 0.0 collective-permute-done.refs_1_
  11.7 0.8 %collective-permute-start.5 = (bf16[16,1280]{1,0:T(8,128)(2,1)S(1)}, bf16[16,1280]{1,0:T(8,128)(2,1)S(1)}, u32[]{:S(2)}, u32[]{:S(2)}) collective-permute-start(bf16[16,1280]{1,0:T(8,128)(2,1)S(1)} %collective-permute-done.1.refs_2_), channel_id=1, source_target_pairs={{0,2},{1,3},{2,0},{3,1},{4,6},{5,7},{6,4},{7,5},{8,10},{9,11},{10,... | collective-permute-start | bytes 122888 | tf_op jit(solution)/shard_map/ppermute | solution.py:214
  12.6 1.4 %prep.1 = (s32[8,128]{1,0:T(8,128)S(1)}, bf16[384,1280]{1,0:T(8,128)(2,1)S(1)}, bf16[16,1280]{1,0:T(8,128)(2,1)S(1)}) custom-call(s32[2,256]{1,0:T(2,128)} %refs_0_.1, s32[1,256]{1,0:T(1,128)} %bitcast.4, s32[1,256]{1,0:T(1,128)} %bitcast.5, s32[1,256]{1,0:T(1,128)} %bitcast.6, s32[5,256]{1,0:T(8,128)} %refs_4_.1, bf16[384,1280]{1,0:T(8,128)(2,1)} %refs_5_.1, ...), custom_call_target="tpu_custom_call" | custom-call | tf_op jit(solution)/shard_map/prep/pallas_call | solution.py:228
  13.9 0.0 collective-permute-done.4.refs_5_
  13.9 0.0 collective-permute-done.3.refs_4_
  14.0 0.3 %collective-permute-done.6.refs_7_ = bf16[16,1280]{1,0:T(8,128)(2,1)S(1)} collective-permute-done((bf16[16,1280]{1,0:T(8,128)(2,1)S(1)}, bf16[16,1280]{1,0:T(8,128)(2,1)S(1)}, u32[]{:S(2)}, u32[]{:S(2)}) %collective-permute-start.6) | collective-permute-done | bytes 40992 | tf_op jit(solution)/shard_map/ppermute | solution.py:214
  14.2 1.5 %collective-permute-done.5.refs_6_ = bf16[16,1280]{1,0:T(8,128)(2,1)S(1)} collective-permute-done((bf16[16,1280]{1,0:T(8,128)(2,1)S(1)}, bf16[16,1280]{1,0:T(8,128)(2,1)S(1)}, u32[]{:S(2)}, u32[]{:S(2)}) %collective-permute-start.5) | collective-permute-done | bytes 40992 | tf_op jit(solution)/shard_map/ppermute | solution.py:214
  15.7 0.0 collective-permute-done.7.refs_9_
  15.7 1.2 %stats.1 = f32[8,1,128]{2,1,0:T(1,128)S(1)} custom-call(bf16[16,1280]{1,0:T(8,128)(2,1)S(1)} %get-tuple-element.7.refs_0_, bf16[16,1280]{1,0:T(8,128)(2,1)S(1)} %collective-permute-done.refs_1_, bf16[16,1280]{1,0:T(8,128)(2,1)S(1)} %collective-permute-done.1.refs_2_, bf16[16,1280]{1,0:T(8,128)(2,1)S(1)} %collective-permute-done.2.refs_3_, ...), custom_call_target="tpu_custom_call" | custom-call | tf_op jit(solution)/shard_map/stats/pallas_call | solution.py:244
  17.0 10.5 %all_to_all.5.got = f32[8,1,128]{2,1,0:T(1,128)S(1)} all-to-all(f32[8,1,128]{2,1,0:T(1,128)S(1)} %stats.1), channel_id=1, replica_groups={{0,2,4,6,8,10,12,14},{1,3,5,7,9,11,13,15},{16,18,20,22,24,26,28,30},{17..., dimensions={0} | all-to-all | bytes 8192 | tf_op jit(solution)/shard_map/all_to_all | solution.py:251
  27.5 0.7 %final.1 = (f32[5,16]{1,0:T(8,128)}, f32[1,16]{1,0:T(1,128)}) custom-call(f32[8,1,128]{2,1,0:T(1,128)S(1)} %all_to_all.5.got, s32[8,128]{1,0:T(8,128)S(1)} %get-tuple-element.9.refs_10_.limits), custom_call_target="tpu_custom_call" | custom-call | tf_op jit(solution)/shard_map/final/pallas_call | solution.py:252
Async XLA Ops:
  0.6 15.1 %collective-permute-start.7 = (bf16[384,1280]{1,0:T(8,128)(2,1)}, bf16[384,1280]{1,0:T(8,128)(2,1)S(1)}, u32[]{:S(2)}, u32[]{:S(2)}) collective-permute-start(bf16[384,1280]{1,0:T(8,128)(2,1)} %refs_5_.1), channel_id=1, source_target_pairs={{0,1},{1,0},{2,3},{3,2},{4,5},{5,4},{6,7},{7,6},{8,9},{9,8},{10,11... | collective-permute-start | bytes 2949128 | tf_op jit(solution)/shard_map/ppermute | solution.py:226
  1.2 7.9 %collective-permute-start.2 = (bf16[16,1280]{1,0:T(8,128)(2,1)}, bf16[16,1280]{1,0:T(8,128)(2,1)S(1)}, u32[]{:S(2)}, u32[]{:S(2)}) collective-permute-start(bf16[16,1280]{1,0:T(8,128)(2,1)} %refs_6_.1), channel_id=1, source_target_pairs={{0,4},{1,5},{2,6},{3,7},{4,8},{5,9},{6,10},{7,11},{8,12},{9,13},{1... | collective-permute-start | bytes 122888 | tf_op jit(solution)/shard_map/ppermute | solution.py:214
  3.8 6.4 %collective-permute-start.1 = (bf16[16,1280]{1,0:T(8,128)(2,1)}, bf16[16,1280]{1,0:T(8,128)(2,1)S(1)}, u32[]{:S(2)}, u32[]{:S(2)}) collective-permute-start(bf16[16,1280]{1,0:T(8,128)(2,1)} %refs_6_.1), channel_id=1, source_target_pairs={{0,8},{1,9},{2,10},{3,11},{4,12},{5,13},{6,14},{7,15},{8,0},{9,1},... | collective-permute-start | bytes 122888 | tf_op jit(solution)/shard_map/ppermute | solution.py:214
  6.4 5.3 %collective-permute-start = (bf16[16,1280]{1,0:T(8,128)(2,1)}, bf16[16,1280]{1,0:T(8,128)(2,1)S(1)}, u32[]{:S(2)}, u32[]{:S(2)}) collective-permute-start(bf16[16,1280]{1,0:T(8,128)(2,1)} %refs_6_.1), channel_id=1, source_target_pairs={{0,12},{1,13},{2,14},{3,15},{4,0},{5,1},{6,2},{7,3},{8,4},{9,5},{1... | collective-permute-start | bytes 122888 | tf_op jit(solution)/shard_map/ppermute | solution.py:214
  7.8 6.2 %collective-permute-start.4 = (bf16[16,1280]{1,0:T(8,128)(2,1)}, bf16[16,1280]{1,0:T(8,128)(2,1)S(1)}, u32[]{:S(2)}, u32[]{:S(2)}) collective-permute-start(bf16[16,1280]{1,0:T(8,128)(2,1)} %refs_6_.1), channel_id=1, source_target_pairs={{0,14},{1,15},{2,12},{3,13},{4,2},{5,3},{6,0},{7,1},{8,6},{9,7},{1... | collective-permute-start | bytes 122888 | tf_op jit(solution)/shard_map/ppermute | solution.py:214
  9.1 4.8 %collective-permute-start.3 = (bf16[16,1280]{1,0:T(8,128)(2,1)}, bf16[16,1280]{1,0:T(8,128)(2,1)S(1)}, u32[]{:S(2)}, u32[]{:S(2)}) collective-permute-start(bf16[16,1280]{1,0:T(8,128)(2,1)} %refs_6_.1), channel_id=1, source_target_pairs={{0,2},{1,3},{2,0},{3,1},{4,6},{5,7},{6,4},{7,5},{8,10},{9,11},{10,... | collective-permute-start | bytes 122888 | tf_op jit(solution)/shard_map/ppermute | solution.py:214
  10.2 4.0 %collective-permute-start.6 = (bf16[16,1280]{1,0:T(8,128)(2,1)S(1)}, bf16[16,1280]{1,0:T(8,128)(2,1)S(1)}, u32[]{:S(2)}, u32[]{:S(2)}) collective-permute-start(bf16[16,1280]{1,0:T(8,128)(2,1)S(1)} %collective-permute-done.2.refs_3_), channel_id=1, source_target_pairs={{0,2},{1,3},{2,0},{3,1},{4,6},{5,7},{6,4},{7,5},{8,10},{9,11},{10,... | collective-permute-start | bytes 122888 | tf_op jit(solution)/shard_map/ppermute | solution.py:214
  11.7 4.0 %collective-permute-start.5 = (bf16[16,1280]{1,0:T(8,128)(2,1)S(1)}, bf16[16,1280]{1,0:T(8,128)(2,1)S(1)}, u32[]{:S(2)}, u32[]{:S(2)}) collective-permute-start(bf16[16,1280]{1,0:T(8,128)(2,1)S(1)} %collective-permute-done.1.refs_2_), channel_id=1, source_target_pairs={{0,2},{1,3},{2,0},{3,1},{4,6},{5,7},{6,4},{7,5},{8,10},{9,11},{10,... | collective-permute-start | bytes 122888 | tf_op jit(solution)/shard_map/ppermute | solution.py:214

commit v2 on v1

--- a/solution.py
+++ b/solution.py
@@ -107,11 +107,13 @@
         text_low, stamp_low, stamp_high = lim[0:1], lim[1:2], lim[2:3]
         picked = [jnp.zeros(block, jnp.float32) for _ in range(FIELDS - 3)]
         segments = []
-        for ref, shard in ((table, index), (other, index ^ 1)):
+        both = lax.dot_general(
+            jnp.concatenate([table[...], other[...]], axis=0), rows, (((1,), (1,)), ((), ())),
+            preferred_element_type=jnp.float32,
+        )
+        for half, shard in enumerate((index, index ^ 1)):
             base = shard * width
-            logits = lax.dot_general(
-                ref[...], rows, (((1,), (1,)), ((), ())), preferred_element_type=jnp.float32
-            )
+            logits = both[half * width:(half + 1) * width]
             wanted = [wide(lim[3 + k:4 + k] - base) for k in range(FIELDS - 3)]
             for first, last in zip((0, edge_at, edge_at + SUBLANES), (edge_at, edge_at + SUBLANES, width)):
                 if first == last:
@@ -163,7 +165,8 @@
         for place in range(per_tile):
             piece = tile * per_tile + (-place) % per_tile
             target = source_of(piece, member, outer)
-            out[pl.ds(target, 1)] = packed[place:place + 1].reshape(1, 1, LANES)
+            slot = lax.rem(target + members // 2, members)
+            out[pl.ds(slot, 1)] = packed[place:place + 1].reshape(1, 1, LANES)
 
     if outer > NEAR:
         @pl.loop(0, members // per_tile)
@@ -247,7 +250,8 @@
         name="stats",
         compiler_params=pltpu.CompilerParams(vmem_limit_bytes=GRANT),
     )(*parts, table, other, limits)
-    same_core = [[2 * i + core for i in range(members)] for core in range(2)]
+    order = [(i + members // 2) % members for i in range(members)]
+    same_core = [[2 * i + core for i in order] for core in range(2)]
     got = lax.all_to_all(stats, "vocab", 0, 0, axis_index_groups=same_core, tiled=True)
     picked, stamped = pl.pallas_call(
         functools.partial(final_kernel, row_dev, stamp_begin),

time: 28.4 us -> 26.5 us (0.933)
  blocking collectives: 10.5 us -> 8.72 us
    all_to_all x1, blocking collectives: 10.5 us -> 8.72 us  [per_device(): lax.all_to_all(stats, 'vocab', 0, 0, axis_index_groups=same_core, tiled=T...]
where the time goes in v2:
time: 26.5 us; the launch traced here: 26.3 us
  starting transfers between devices  11.5 us (43%)
  blocking collectives  8.72 us (33%)
  Pallas kernels  3.23 us (12%)
  waiting for transfers between devices  2.26 us (9%)
  between operations  0.67 us (3%)
    ppermute x7, starting transfers between devices, move(): return lax.ppermute(array, 'vocab', pairs)  10.9 us
    all_to_all x1, blocking collectives, per_device(): lax.all_to_all(stats, 'vocab', 0, 0, axis_index_groups=same_core, tiled=T...  8.72 us
    ppermute x7, waiting for transfers between devices, move(): return lax.ppermute(array, 'vocab', pairs)  2.26 us
    pallas_call x1, Pallas kernels, per_device(): pl.pallas_call(functools.partial(prep_kernel, members, row_dev, stamp_beg...  1.37 us
    pallas_call x1, Pallas kernels, per_device(): pl.pallas_call(functools.partial(stats_kernel, members, row_dev, stamp_be...  1.13 us
    pallas_call x1, Pallas kernels, per_device(): pl.pallas_call(functools.partial(final_kernel, row_dev, stamp_begin), out...  0.73 us
    ppermute x1, starting transfers between devices, per_device(): other = lax.ppermute(embedding, 'vocab', [(i, i ^ 1) for i in range(count)])  0.56 us
  transfers between devices with their start and end apart: 8, of which 3 were waited for; matrix products, arithmetic and copies ran while one was open for 0% of the time, Pallas kernels for 5%

profile of v2, /device:TPU:0, one launch (start us, length us, event | category | flops | bytes accessed | tf_op | source)
XLA Modules:
  0.0 26.3 jit_solution(14687459453664910696)
XLA Ops:
  0.6 0.6 %collective-permute-start.7 = (bf16[384,1280]{1,0:T(8,128)(2,1)}, bf16[384,1280]{1,0:T(8,128)(2,1)S(1)}, u32[]{:S(2)}, u32[]{:S(2)}) collective-permute-start(bf16[384,1280]{1,0:T(8,128)(2,1)} %refs_5_.1), channel_id=1, source_target_pairs={{0,1},{1,0},{2,3},{3,2},{4,5},{5,4},{6,7},{7,6},{8,9},{9,8},{10,11... | collective-permute-start | bytes 2949128 | tf_op jit(solution)/shard_map/ppermute | solution.py:229
  1.2 2.6 %collective-permute-start.2 = (bf16[16,1280]{1,0:T(8,128)(2,1)}, bf16[16,1280]{1,0:T(8,128)(2,1)S(1)}, u32[]{:S(2)}, u32[]{:S(2)}) collective-permute-start(bf16[16,1280]{1,0:T(8,128)(2,1)} %refs_6_.1), channel_id=1, source_target_pairs={{0,4},{1,5},{2,6},{3,7},{4,8},{5,9},{6,10},{7,11},{8,12},{9,13},{1... | collective-permute-start | bytes 122888 | tf_op jit(solution)/shard_map/ppermute | solution.py:217
  3.8 2.6 %collective-permute-start.1 = (bf16[16,1280]{1,0:T(8,128)(2,1)}, bf16[16,1280]{1,0:T(8,128)(2,1)S(1)}, u32[]{:S(2)}, u32[]{:S(2)}) collective-permute-start(bf16[16,1280]{1,0:T(8,128)(2,1)} %refs_6_.1), channel_id=1, source_target_pairs={{0,8},{1,9},{2,10},{3,11},{4,12},{5,13},{6,14},{7,15},{8,0},{9,1},... | collective-permute-start | bytes 122888 | tf_op jit(solution)/shard_map/ppermute | solution.py:217
  6.4 1.3 %collective-permute-start = (bf16[16,1280]{1,0:T(8,128)(2,1)}, bf16[16,1280]{1,0:T(8,128)(2,1)S(1)}, u32[]{:S(2)}, u32[]{:S(2)}) collective-permute-start(bf16[16,1280]{1,0:T(8,128)(2,1)} %refs_6_.1), channel_id=1, source_target_pairs={{0,12},{1,13},{2,14},{3,15},{4,0},{5,1},{6,2},{7,3},{8,4},{9,5},{1... | collective-permute-start | bytes 122888 | tf_op jit(solution)/shard_map/ppermute | solution.py:217
  7.8 1.4 %collective-permute-start.4 = (bf16[16,1280]{1,0:T(8,128)(2,1)}, bf16[16,1280]{1,0:T(8,128)(2,1)S(1)}, u32[]{:S(2)}, u32[]{:S(2)}) collective-permute-start(bf16[16,1280]{1,0:T(8,128)(2,1)} %refs_6_.1), channel_id=1, source_target_pairs={{0,14},{1,15},{2,12},{3,13},{4,2},{5,3},{6,0},{7,1},{8,6},{9,7},{1... | collective-permute-start | bytes 122888 | tf_op jit(solution)/shard_map/ppermute | solution.py:217
  9.1 0.0 collective-permute-done.2.refs_3_
  9.1 0.7 %collective-permute-start.3 = (bf16[16,1280]{1,0:T(8,128)(2,1)}, bf16[16,1280]{1,0:T(8,128)(2,1)S(1)}, u32[]{:S(2)}, u32[]{:S(2)}) collective-permute-start(bf16[16,1280]{1,0:T(8,128)(2,1)} %refs_6_.1), channel_id=1, source_target_pairs={{0,2},{1,3},{2,0},{3,1},{4,6},{5,7},{6,4},{7,5},{8,10},{9,11},{10,... | collective-permute-start | bytes 122888 | tf_op jit(solution)/shard_map/ppermute | solution.py:217
  9.8 0.5 %collective-permute-done.1.refs_2_ = bf16[16,1280]{1,0:T(8,128)(2,1)S(1)} collective-permute-done((bf16[16,1280]{1,0:T(8,128)(2,1)}, bf16[16,1280]{1,0:T(8,128)(2,1)S(1)}, u32[]{:S(2)}, u32[]{:S(2)}) %collective-permute-start.1) | collective-permute-done | bytes 40992 | tf_op jit(solution)/shard_map/ppermute | solution.py:217
  10.2 1.5 %collective-permute-start.6 = (bf16[16,1280]{1,0:T(8,128)(2,1)S(1)}, bf16[16,1280]{1,0:T(8,128)(2,1)S(1)}, u32[]{:S(2)}, u32[]{:S(2)}) collective-permute-start(bf16[16,1280]{1,0:T(8,128)(2,1)S(1)} %collective-permute-done.2.refs_3_), channel_id=1, source_target_pairs={{0,2},{1,3},{2,0},{3,1},{4,6},{5,7},{6,4},{7,5},{8,10},{9,11},{10,... | collective-permute-start | bytes 122888 | tf_op jit(solution)/shard_map/ppermute | solution.py:217
  11.7 0.0 collective-permute-done.refs_1_
  11.7 0.8 %collective-permute-start.5 = (bf16[16,1280]{1,0:T(8,128)(2,1)S(1)}, bf16[16,1280]{1,0:T(8,128)(2,1)S(1)}, u32[]{:S(2)}, u32[]{:S(2)}) collective-permute-start(bf16[16,1280]{1,0:T(8,128)(2,1)S(1)} %collective-permute-done.1.refs_2_), channel_id=1, source_target_pairs={{0,2},{1,3},{2,0},{3,1},{4,6},{5,7},{6,4},{7,5},{8,10},{9,11},{10,... | collective-permute-start | bytes 122888 | tf_op jit(solution)/shard_map/ppermute | solution.py:217
  12.6 1.4 %prep.1 = (s32[8,128]{1,0:T(8,128)S(1)}, bf16[384,1280]{1,0:T(8,128)(2,1)S(1)}, bf16[16,1280]{1,0:T(8,128)(2,1)S(1)}) custom-call(s32[2,256]{1,0:T(2,128)} %refs_0_.1, s32[1,256]{1,0:T(1,128)} %bitcast.4, s32[1,256]{1,0:T(1,128)} %bitcast.5, s32[1,256]{1,0:T(1,128)} %bitcast.6, s32[5,256]{1,0:T(8,128)} %refs_4_.1, bf16[384,1280]{1,0:T(8,128)(2,1)} %refs_5_.1, ...), custom_call_target="tpu_custom_call" | custom-call | tf_op jit(solution)/shard_map/prep/pallas_call | solution.py:231
  13.9 0.0 collective-permute-done.4.refs_5_
  13.9 0.0 collective-permute-done.3.refs_4_
  14.0 0.3 %collective-permute-done.6.refs_7_ = bf16[16,1280]{1,0:T(8,128)(2,1)S(1)} collective-permute-done((bf16[16,1280]{1,0:T(8,128)(2,1)S(1)}, bf16[16,1280]{1,0:T(8,128)(2,1)S(1)}, u32[]{:S(2)}, u32[]{:S(2)}) %collective-permute-start.6) | collective-permute-done | bytes 40992 | tf_op jit(solution)/shard_map/ppermute | solution.py:217
  14.2 1.5 %collective-permute-done.5.refs_6_ = bf16[16,1280]{1,0:T(8,128)(2,1)S(1)} collective-permute-done((bf16[16,1280]{1,0:T(8,128)(2,1)S(1)}, bf16[16,1280]{1,0:T(8,128)(2,1)S(1)}, u32[]{:S(2)}, u32[]{:S(2)}) %collective-permute-start.5) | collective-permute-done | bytes 40992 | tf_op jit(solution)/shard_map/ppermute | solution.py:217
  15.7 0.0 collective-permute-done.7.refs_9_
  15.7 1.1 %stats.1 = f32[8,1,128]{2,1,0:T(1,128)S(1)} custom-call(bf16[16,1280]{1,0:T(8,128)(2,1)S(1)} %get-tuple-element.7.refs_0_, bf16[16,1280]{1,0:T(8,128)(2,1)S(1)} %collective-permute-done.refs_1_, bf16[16,1280]{1,0:T(8,128)(2,1)S(1)} %collective-permute-done.1.refs_2_, bf16[16,1280]{1,0:T(8,128)(2,1)S(1)} %collective-permute-done.2.refs_3_, ...), custom_call_target="tpu_custom_call" | custom-call | tf_op jit(solution)/shard_map/stats/pallas_call | solution.py:247
  16.9 8.7 %all_to_all.5.got = f32[8,1,128]{2,1,0:T(1,128)S(1)} all-to-all(f32[8,1,128]{2,1,0:T(1,128)S(1)} %stats.1), channel_id=1, replica_groups={{8,10,12,14,0,2,4,6},{9,11,13,15,1,3,5,7},{24,26,28,30,16,18,20,22},{25..., dimensions={0} | all-to-all | bytes 8192 | tf_op jit(solution)/shard_map/all_to_all | solution.py:255
  25.6 0.7 %final.1 = (f32[5,16]{1,0:T(8,128)}, f32[1,16]{1,0:T(1,128)}) custom-call(f32[8,1,128]{2,1,0:T(1,128)S(1)} %all_to_all.5.got, s32[8,128]{1,0:T(8,128)S(1)} %get-tuple-element.9.refs_10_.limits), custom_call_target="tpu_custom_call" | custom-call | tf_op jit(solution)/shard_map/final/pallas_call | solution.py:256
Async XLA Ops:
  0.6 15.1 %collective-permute-start.7 = (bf16[384,1280]{1,0:T(8,128)(2,1)}, bf16[384,1280]{1,0:T(8,128)(2,1)S(1)}, u32[]{:S(2)}, u32[]{:S(2)}) collective-permute-start(bf16[384,1280]{1,0:T(8,128)(2,1)} %refs_5_.1), channel_id=1, source_target_pairs={{0,1},{1,0},{2,3},{3,2},{4,5},{5,4},{6,7},{7,6},{8,9},{9,8},{10,11... | collective-permute-start | bytes 2949128 | tf_op jit(solution)/shard_map/ppermute | solution.py:229
  1.2 7.9 %collective-permute-start.2 = (bf16[16,1280]{1,0:T(8,128)(2,1)}, bf16[16,1280]{1,0:T(8,128)(2,1)S(1)}, u32[]{:S(2)}, u32[]{:S(2)}) collective-permute-start(bf16[16,1280]{1,0:T(8,128)(2,1)} %refs_6_.1), channel_id=1, source_target_pairs={{0,4},{1,5},{2,6},{3,7},{4,8},{5,9},{6,10},{7,11},{8,12},{9,13},{1... | collective-permute-start | bytes 122888 | tf_op jit(solution)/shard_map/ppermute | solution.py:217
  3.8 6.4 %collective-permute-start.1 = (bf16[16,1280]{1,0:T(8,128)(2,1)}, bf16[16,1280]{1,0:T(8,128)(2,1)S(1)}, u32[]{:S(2)}, u32[]{:S(2)}) collective-permute-start(bf16[16,1280]{1,0:T(8,128)(2,1)} %refs_6_.1), channel_id=1, source_target_pairs={{0,8},{1,9},{2,10},{3,11},{4,12},{5,13},{6,14},{7,15},{8,0},{9,1},... | collective-permute-start | bytes 122888 | tf_op jit(solution)/shard_map/ppermute | solution.py:217
  6.4 5.3 %collective-permute-start = (bf16[16,1280]{1,0:T(8,128)(2,1)}, bf16[16,1280]{1,0:T(8,128)(2,1)S(1)}, u32[]{:S(2)}, u32[]{:S(2)}) collective-permute-start(bf16[16,1280]{1,0:T(8,128)(2,1)} %refs_6_.1), channel_id=1, source_target_pairs={{0,12},{1,13},{2,14},{3,15},{4,0},{5,1},{6,2},{7,3},{8,4},{9,5},{1... | collective-permute-start | bytes 122888 | tf_op jit(solution)/shard_map/ppermute | solution.py:217
  7.8 6.2 %collective-permute-start.4 = (bf16[16,1280]{1,0:T(8,128)(2,1)}, bf16[16,1280]{1,0:T(8,128)(2,1)S(1)}, u32[]{:S(2)}, u32[]{:S(2)}) collective-permute-start(bf16[16,1280]{1,0:T(8,128)(2,1)} %refs_6_.1), channel_id=1, source_target_pairs={{0,14},{1,15},{2,12},{3,13},{4,2},{5,3},{6,0},{7,1},{8,6},{9,7},{1... | collective-permute-start | bytes 122888 | tf_op jit(solution)/shard_map/ppermute | solution.py:217
  9.1 4.8 %collective-permute-start.3 = (bf16[16,1280]{1,0:T(8,128)(2,1)}, bf16[16,1280]{1,0:T(8,128)(2,1)S(1)}, u32[]{:S(2)}, u32[]{:S(2)}) collective-permute-start(bf16[16,1280]{1,0:T(8,128)(2,1)} %refs_6_.1), channel_id=1, source_target_pairs={{0,2},{1,3},{2,0},{3,1},{4,6},{5,7},{6,4},{7,5},{8,10},{9,11},{10,... | collective-permute-start | bytes 122888 | tf_op jit(solution)/shard_map/ppermute | solution.py:217
  10.2 4.0 %collective-permute-start.6 = (bf16[16,1280]{1,0:T(8,128)(2,1)S(1)}, bf16[16,1280]{1,0:T(8,128)(2,1)S(1)}, u32[]{:S(2)}, u32[]{:S(2)}) collective-permute-start(bf16[16,1280]{1,0:T(8,128)(2,1)S(1)} %collective-permute-done.2.refs_3_), channel_id=1, source_target_pairs={{0,2},{1,3},{2,0},{3,1},{4,6},{5,7},{6,4},{7,5},{8,10},{9,11},{10,... | collective-permute-start | bytes 122888 | tf_op jit(solution)/shard_map/ppermute | solution.py:217
  11.7 4.0 %collective-permute-start.5 = (bf16[16,1280]{1,0:T(8,128)(2,1)S(1)}, bf16[16,1280]{1,0:T(8,128)(2,1)S(1)}, u32[]{:S(2)}, u32[]{:S(2)}) collective-permute-start(bf16[16,1280]{1,0:T(8,128)(2,1)S(1)} %collective-permute-done.1.refs_2_), channel_id=1, source_target_pairs={{0,2},{1,3},{2,0},{3,1},{4,6},{5,7},{6,4},{7,5},{8,10},{9,11},{10,... | collective-permute-start | bytes 122888 | tf_op jit(solution)/shard_map/ppermute | solution.py:217

commit v3 on v2

--- a/solution.py
+++ b/solution.py
@@ -67,23 +67,29 @@
     index = lax.axis_index("vocab")
     per_tile = LANES // row_dev
     lane = lax.broadcasted_iota(jnp.int32, (FIELDS, LANES), 1)
+
+    def moved(owner, place):
+        source = 2 * owner + lax.rem(index, 2)
+        at = pl.multiple_of(lax.div(source, per_tile) * LANES, LANES)
+        span = pl.ds(at, LANES)
+        limits = row_limits(
+            prev[0:1, span], prev[1:2, span], stamp[:, span], begin[:, span], length[:, span],
+            stamp_begin,
+        )
+        fields = jnp.concatenate(list(limits) + [chosen[:, span]], axis=0)
+        shift = lax.rem(place - lax.rem(source, per_tile) + per_tile, per_tile) * row_dev
+        return pltpu.roll(fields, shift, 1)
+
+    member = lax.div(index, 2)
     for tile in range(members // per_tile):
         total = jnp.zeros((FIELDS, LANES), jnp.int32)
         for place in range(per_tile):
-            owner = source_of(tile * per_tile + place, lax.div(index, 2), members // 2)
-            source = 2 * owner + lax.rem(index, 2)
-            at = pl.multiple_of(lax.div(source, per_tile) * LANES, LANES)
-            span = pl.ds(at, LANES)
-            limits = row_limits(
-                prev[0:1, span], prev[1:2, span], stamp[:, span], begin[:, span], length[:, span],
-                stamp_begin,
-            )
-            fields = jnp.concatenate(list(limits) + [chosen[:, span]], axis=0)
-            shift = lax.rem(place - lax.rem(source, per_tile) + per_tile, per_tile) * row_dev
-            moved = pltpu.roll(fields, shift, 1)
             here = (lane >= place * row_dev) & (lane < (place + 1) * row_dev)
-            total = jnp.where(here, moved, total)
+            owner = source_of(tile * per_tile + place, member, members // 2)
+            total = jnp.where(here, moved(owner, place), total)
         out[:, tile * LANES:(tile + 1) * LANES] = total
+    if members // 2 > NEAR:
+        out[:, members * row_dev:] = moved(member, 0)
     for copy in copies[5:]:
         copy.wait()
 
@@ -180,7 +186,7 @@
             tile_stats(rows[span], limits[:, span], tile)
 
 
-def final_kernel(row_dev, stamp_begin, got, limits, picked_out, stamp_out):
+def final_kernel(row_dev, stamp_begin, own_at, got, limits, picked_out, stamp_out):
     parts = got[:, 0, :]
     top = jnp.max(parts, axis=0, keepdims=True)
     lse = top + jnp.log(jnp.sum(jnp.exp(parts - top), axis=0, keepdims=True))
@@ -195,7 +201,7 @@
     shifted = text_lse - penalty
     larger = jnp.maximum(shifted, stamp_lse)
     total = larger + jnp.log(jnp.exp(shifted - larger) + jnp.exp(stamp_lse - larger))
-    chosen = limits[:, 0:LANES]
+    chosen = limits[:, own_at:own_at + LANES]
     adjusted = fields - jnp.where(chosen < stamp_begin, penalty, 0.0) - total
     result = jnp.maximum(adjusted, FLOOR)
     picked_out[...] = result[3:, :row_dev]
@@ -211,6 +217,7 @@
     outer = members // 2
     stamp_begin = width * count - TSN
     core_rows = members * row_dev
+    own_at = core_rows if outer > NEAR else 0
 
     def move(array, step, side):
         pairs = [(i, ((i - 4 * step) % count) ^ (2 * side)) for i in range(count)]
@@ -233,7 +240,7 @@
         in_specs=[pl.BlockSpec(memory_space=pltpu.HBM)] * 7,
         out_specs=[pl.BlockSpec(memory_space=pltpu.VMEM)] * 3,
         out_shape=(
-            jax.ShapeDtypeStruct((FIELDS, core_rows), jnp.int32),
+            jax.ShapeDtypeStruct((FIELDS, max(core_rows, own_at + LANES)), jnp.int32),
             jax.ShapeDtypeStruct(embedding.shape, embedding.dtype),
             jax.ShapeDtypeStruct(hidden.shape, hidden.dtype),
         ),
@@ -254,7 +261,7 @@
     same_core = [[2 * i + core for i in order] for core in range(2)]
     got = lax.all_to_all(stats, "vocab", 0, 0, axis_index_groups=same_core, tiled=True)
     picked, stamped = pl.pallas_call(
-        functools.partial(final_kernel, row_dev, stamp_begin),
+        functools.partial(final_kernel, row_dev, stamp_begin, own_at),
         out_shape=(
             jax.ShapeDtypeStruct((nsel, row_dev), jnp.float32),
             jax.ShapeDtypeStruct((1, row_dev), jnp.float32),

time: 26.5 us -> 26.5 us (level)
  no operation moved by 1% of the time
where the time goes in v3:
time: 26.5 us; the launch traced here: 26.3 us
  starting transfers between devices  11.5 us (43%)
  blocking collectives  8.72 us (33%)
  Pallas kernels  3.23 us (12%)
  waiting for transfers between devices  2.26 us (9%)
  between operations  0.67 us (3%)
    ppermute x7, starting transfers between devices, move(): return lax.ppermute(array, 'vocab', pairs)  10.9 us
    all_to_all x1, blocking collectives, per_device(): lax.all_to_all(stats, 'vocab', 0, 0, axis_index_groups=same_core, tiled=T...  8.72 us
    ppermute x7, waiting for transfers between devices, move(): return lax.ppermute(array, 'vocab', pairs)  2.26 us
    pallas_call x1, Pallas kernels, per_device(): pl.pallas_call(functools.partial(prep_kernel, members, row_dev, stamp_beg...  1.37 us
    pallas_call x1, Pallas kernels, per_device(): pl.pallas_call(functools.partial(stats_kernel, members, row_dev, stamp_be...  1.13 us
    pallas_call x1, Pallas kernels, per_device(): pl.pallas_call(functools.partial(final_kernel, row_dev, stamp_begin, own_...  0.73 us
    ppermute x1, starting transfers between devices, per_device(): other = lax.ppermute(embedding, 'vocab', [(i, i ^ 1) for i in range(count)])  0.56 us
  transfers between devices with their start and end apart: 8, of which 3 were waited for; matrix products, arithmetic and copies ran while one was open for 0% of the time, Pallas kernels for 5%

profile of v3, /device:TPU:0, one launch (start us, length us, event | category | flops | bytes accessed | tf_op | source)
XLA Modules:
  0.0 26.3 jit_solution(14687459453664910696)
XLA Ops:
  0.6 0.6 %collective-permute-start.7 = (bf16[384,1280]{1,0:T(8,128)(2,1)}, bf16[384,1280]{1,0:T(8,128)(2,1)S(1)}, u32[]{:S(2)}, u32[]{:S(2)}) collective-permute-start(bf16[384,1280]{1,0:T(8,128)(2,1)} %refs_5_.1), channel_id=1, source_target_pairs={{0,1},{1,0},{2,3},{3,2},{4,5},{5,4},{6,7},{7,6},{8,9},{9,8},{10,11... | collective-permute-start | bytes 2949128 | tf_op jit(solution)/shard_map/ppermute | solution.py:236
  1.2 2.6 %collective-permute-start.2 = (bf16[16,1280]{1,0:T(8,128)(2,1)}, bf16[16,1280]{1,0:T(8,128)(2,1)S(1)}, u32[]{:S(2)}, u32[]{:S(2)}) collective-permute-start(bf16[16,1280]{1,0:T(8,128)(2,1)} %refs_6_.1), channel_id=1, source_target_pairs={{0,4},{1,5},{2,6},{3,7},{4,8},{5,9},{6,10},{7,11},{8,12},{9,13},{1... | collective-permute-start | bytes 122888 | tf_op jit(solution)/shard_map/ppermute | solution.py:224
  3.8 2.6 %collective-permute-start.1 = (bf16[16,1280]{1,0:T(8,128)(2,1)}, bf16[16,1280]{1,0:T(8,128)(2,1)S(1)}, u32[]{:S(2)}, u32[]{:S(2)}) collective-permute-start(bf16[16,1280]{1,0:T(8,128)(2,1)} %refs_6_.1), channel_id=1, source_target_pairs={{0,8},{1,9},{2,10},{3,11},{4,12},{5,13},{6,14},{7,15},{8,0},{9,1},... | collective-permute-start | bytes 122888 | tf_op jit(solution)/shard_map/ppermute | solution.py:224
  6.4 1.3 %collective-permute-start = (bf16[16,1280]{1,0:T(8,128)(2,1)}, bf16[16,1280]{1,0:T(8,128)(2,1)S(1)}, u32[]{:S(2)}, u32[]{:S(2)}) collective-permute-start(bf16[16,1280]{1,0:T(8,128)(2,1)} %refs_6_.1), channel_id=1, source_target_pairs={{0,12},{1,13},{2,14},{3,15},{4,0},{5,1},{6,2},{7,3},{8,4},{9,5},{1... | collective-permute-start | bytes 122888 | tf_op jit(solution)/shard_map/ppermute | solution.py:224
  7.8 1.4 %collective-permute-start.4 = (bf16[16,1280]{1,0:T(8,128)(2,1)}, bf16[16,1280]{1,0:T(8,128)(2,1)S(1)}, u32[]{:S(2)}, u32[]{:S(2)}) collective-permute-start(bf16[16,1280]{1,0:T(8,128)(2,1)} %refs_6_.1), channel_id=1, source_target_pairs={{0,14},{1,15},{2,12},{3,13},{4,2},{5,3},{6,0},{7,1},{8,6},{9,7},{1... | collective-permute-start | bytes 122888 | tf_op jit(solution)/shard_map/ppermute | solution.py:224
  9.1 0.0 collective-permute-done.2.refs_3_
  9.1 0.7 %collective-permute-start.3 = (bf16[16,1280]{1,0:T(8,128)(2,1)}, bf16[16,1280]{1,0:T(8,128)(2,1)S(1)}, u32[]{:S(2)}, u32[]{:S(2)}) collective-permute-start(bf16[16,1280]{1,0:T(8,128)(2,1)} %refs_6_.1), channel_id=1, source_target_pairs={{0,2},{1,3},{2,0},{3,1},{4,6},{5,7},{6,4},{7,5},{8,10},{9,11},{10,... | collective-permute-start | bytes 122888 | tf_op jit(solution)/shard_map/ppermute | solution.py:224
  9.8 0.5 %collective-permute-done.1.refs_2_ = bf16[16,1280]{1,0:T(8,128)(2,1)S(1)} collective-permute-done((bf16[16,1280]{1,0:T(8,128)(2,1)}, bf16[16,1280]{1,0:T(8,128)(2,1)S(1)}, u32[]{:S(2)}, u32[]{:S(2)}) %collective-permute-start.1) | collective-permute-done | bytes 40992 | tf_op jit(solution)/shard_map/ppermute | solution.py:224
  10.2 1.5 %collective-permute-start.6 = (bf16[16,1280]{1,0:T(8,128)(2,1)S(1)}, bf16[16,1280]{1,0:T(8,128)(2,1)S(1)}, u32[]{:S(2)}, u32[]{:S(2)}) collective-permute-start(bf16[16,1280]{1,0:T(8,128)(2,1)S(1)} %collective-permute-done.2.refs_3_), channel_id=1, source_target_pairs={{0,2},{1,3},{2,0},{3,1},{4,6},{5,7},{6,4},{7,5},{8,10},{9,11},{10,... | collective-permute-start | bytes 122888 | tf_op jit(solution)/shard_map/ppermute | solution.py:224
  11.7 0.0 collective-permute-done.refs_1_
  11.7 0.8 %collective-permute-start.5 = (bf16[16,1280]{1,0:T(8,128)(2,1)S(1)}, bf16[16,1280]{1,0:T(8,128)(2,1)S(1)}, u32[]{:S(2)}, u32[]{:S(2)}) collective-permute-start(bf16[16,1280]{1,0:T(8,128)(2,1)S(1)} %collective-permute-done.1.refs_2_), channel_id=1, source_target_pairs={{0,2},{1,3},{2,0},{3,1},{4,6},{5,7},{6,4},{7,5},{8,10},{9,11},{10,... | collective-permute-start | bytes 122888 | tf_op jit(solution)/shard_map/ppermute | solution.py:224
  12.6 1.4 %prep.1 = (s32[8,128]{1,0:T(8,128)S(1)}, bf16[384,1280]{1,0:T(8,128)(2,1)S(1)}, bf16[16,1280]{1,0:T(8,128)(2,1)S(1)}) custom-call(s32[2,256]{1,0:T(2,128)} %refs_0_.1, s32[1,256]{1,0:T(1,128)} %bitcast.4, s32[1,256]{1,0:T(1,128)} %bitcast.5, s32[1,256]{1,0:T(1,128)} %bitcast.6, s32[5,256]{1,0:T(8,128)} %refs_4_.1, bf16[384,1280]{1,0:T(8,128)(2,1)} %refs_5_.1, ...), custom_call_target="tpu_custom_call" | custom-call | tf_op jit(solution)/shard_map/prep/pallas_call | solution.py:238
  13.9 0.0 collective-permute-done.4.refs_5_
  13.9 0.0 collective-permute-done.3.refs_4_
  14.0 0.3 %collective-permute-done.6.refs_7_ = bf16[16,1280]{1,0:T(8,128)(2,1)S(1)} collective-permute-done((bf16[16,1280]{1,0:T(8,128)(2,1)S(1)}, bf16[16,1280]{1,0:T(8,128)(2,1)S(1)}, u32[]{:S(2)}, u32[]{:S(2)}) %collective-permute-start.6) | collective-permute-done | bytes 40992 | tf_op jit(solution)/shard_map/ppermute | solution.py:224
  14.2 1.5 %collective-permute-done.5.refs_6_ = bf16[16,1280]{1,0:T(8,128)(2,1)S(1)} collective-permute-done((bf16[16,1280]{1,0:T(8,128)(2,1)S(1)}, bf16[16,1280]{1,0:T(8,128)(2,1)S(1)}, u32[]{:S(2)}, u32[]{:S(2)}) %collective-permute-start.5) | collective-permute-done | bytes 40992 | tf_op jit(solution)/shard_map/ppermute | solution.py:224
  15.7 0.0 collective-permute-done.7.refs_9_
  15.7 1.1 %stats.1 = f32[8,1,128]{2,1,0:T(1,128)S(1)} custom-call(bf16[16,1280]{1,0:T(8,128)(2,1)S(1)} %get-tuple-element.7.refs_0_, bf16[16,1280]{1,0:T(8,128)(2,1)S(1)} %collective-permute-done.refs_1_, bf16[16,1280]{1,0:T(8,128)(2,1)S(1)} %collective-permute-done.1.refs_2_, bf16[16,1280]{1,0:T(8,128)(2,1)S(1)} %collective-permute-done.2.refs_3_, ...), custom_call_target="tpu_custom_call" | custom-call | tf_op jit(solution)/shard_map/stats/pallas_call | solution.py:254
  16.9 8.7 %all_to_all.5.got = f32[8,1,128]{2,1,0:T(1,128)S(1)} all-to-all(f32[8,1,128]{2,1,0:T(1,128)S(1)} %stats.1), channel_id=1, replica_groups={{8,10,12,14,0,2,4,6},{9,11,13,15,1,3,5,7},{24,26,28,30,16,18,20,22},{25..., dimensions={0} | all-to-all | bytes 8192 | tf_op jit(solution)/shard_map/all_to_all | solution.py:262
  25.6 0.7 %final.1 = (f32[5,16]{1,0:T(8,128)}, f32[1,16]{1,0:T(1,128)}) custom-call(f32[8,1,128]{2,1,0:T(1,128)S(1)} %all_to_all.5.got, s32[8,128]{1,0:T(8,128)S(1)} %get-tuple-element.9.refs_10_.limits), custom_call_target="tpu_custom_call" | custom-call | tf_op jit(solution)/shard_map/final/pallas_call | solution.py:263
Async XLA Ops:
  0.6 15.1 %collective-permute-start.7 = (bf16[384,1280]{1,0:T(8,128)(2,1)}, bf16[384,1280]{1,0:T(8,128)(2,1)S(1)}, u32[]{:S(2)}, u32[]{:S(2)}) collective-permute-start(bf16[384,1280]{1,0:T(8,128)(2,1)} %refs_5_.1), channel_id=1, source_target_pairs={{0,1},{1,0},{2,3},{3,2},{4,5},{5,4},{6,7},{7,6},{8,9},{9,8},{10,11... | collective-permute-start | bytes 2949128 | tf_op jit(solution)/shard_map/ppermute | solution.py:236
  1.2 7.9 %collective-permute-start.2 = (bf16[16,1280]{1,0:T(8,128)(2,1)}, bf16[16,1280]{1,0:T(8,128)(2,1)S(1)}, u32[]{:S(2)}, u32[]{:S(2)}) collective-permute-start(bf16[16,1280]{1,0:T(8,128)(2,1)} %refs_6_.1), channel_id=1, source_target_pairs={{0,4},{1,5},{2,6},{3,7},{4,8},{5,9},{6,10},{7,11},{8,12},{9,13},{1... | collective-permute-start | bytes 122888 | tf_op jit(solution)/shard_map/ppermute | solution.py:224
  3.8 6.4 %collective-permute-start.1 = (bf16[16,1280]{1,0:T(8,128)(2,1)}, bf16[16,1280]{1,0:T(8,128)(2,1)S(1)}, u32[]{:S(2)}, u32[]{:S(2)}) collective-permute-start(bf16[16,1280]{1,0:T(8,128)(2,1)} %refs_6_.1), channel_id=1, source_target_pairs={{0,8},{1,9},{2,10},{3,11},{4,12},{5,13},{6,14},{7,15},{8,0},{9,1},... | collective-permute-start | bytes 122888 | tf_op jit(solution)/shard_map/ppermute | solution.py:224
  6.4 5.3 %collective-permute-start = (bf16[16,1280]{1,0:T(8,128)(2,1)}, bf16[16,1280]{1,0:T(8,128)(2,1)S(1)}, u32[]{:S(2)}, u32[]{:S(2)}) collective-permute-start(bf16[16,1280]{1,0:T(8,128)(2,1)} %refs_6_.1), channel_id=1, source_target_pairs={{0,12},{1,13},{2,14},{3,15},{4,0},{5,1},{6,2},{7,3},{8,4},{9,5},{1... | collective-permute-start | bytes 122888 | tf_op jit(solution)/shard_map/ppermute | solution.py:224
  7.8 6.2 %collective-permute-start.4 = (bf16[16,1280]{1,0:T(8,128)(2,1)}, bf16[16,1280]{1,0:T(8,128)(2,1)S(1)}, u32[]{:S(2)}, u32[]{:S(2)}) collective-permute-start(bf16[16,1280]{1,0:T(8,128)(2,1)} %refs_6_.1), channel_id=1, source_target_pairs={{0,14},{1,15},{2,12},{3,13},{4,2},{5,3},{6,0},{7,1},{8,6},{9,7},{1... | collective-permute-start | bytes 122888 | tf_op jit(solution)/shard_map/ppermute | solution.py:224
  9.1 4.8 %collective-permute-start.3 = (bf16[16,1280]{1,0:T(8,128)(2,1)}, bf16[16,1280]{1,0:T(8,128)(2,1)S(1)}, u32[]{:S(2)}, u32[]{:S(2)}) collective-permute-start(bf16[16,1280]{1,0:T(8,128)(2,1)} %refs_6_.1), channel_id=1, source_target_pairs={{0,2},{1,3},{2,0},{3,1},{4,6},{5,7},{6,4},{7,5},{8,10},{9,11},{10,... | collective-permute-start | bytes 122888 | tf_op jit(solution)/shard_map/ppermute | solution.py:224
  10.2 4.0 %collective-permute-start.6 = (bf16[16,1280]{1,0:T(8,128)(2,1)S(1)}, bf16[16,1280]{1,0:T(8,128)(2,1)S(1)}, u32[]{:S(2)}, u32[]{:S(2)}) collective-permute-start(bf16[16,1280]{1,0:T(8,128)(2,1)S(1)} %collective-permute-done.2.refs_3_), channel_id=1, source_target_pairs={{0,2},{1,3},{2,0},{3,1},{4,6},{5,7},{6,4},{7,5},{8,10},{9,11},{10,... | collective-permute-start | bytes 122888 | tf_op jit(solution)/shard_map/ppermute | solution.py:224
  11.7 4.0 %collective-permute-start.5 = (bf16[16,1280]{1,0:T(8,128)(2,1)S(1)}, bf16[16,1280]{1,0:T(8,128)(2,1)S(1)}, u32[]{:S(2)}, u32[]{:S(2)}) collective-permute-start(bf16[16,1280]{1,0:T(8,128)(2,1)S(1)} %collective-permute-done.1.refs_2_), channel_id=1, source_target_pairs={{0,2},{1,3},{2,0},{3,1},{4,6},{5,7},{6,4},{7,5},{8,10},{9,11},{10,... | collective-permute-start | bytes 122888 | tf_op jit(solution)/shard_map/ppermute | solution.py:224

commit v4 on v3

--- a/solution.py
+++ b/solution.py
@@ -24,7 +24,7 @@
 GRANT = 24 << 20
 NEAR = 4
 
-DIRECT = (1,)
+DIRECT = 1
 
 
 def source_of(piece, member, outer):
@@ -171,7 +171,7 @@
         for place in range(per_tile):
             piece = tile * per_tile + (-place) % per_tile
             target = source_of(piece, member, outer)
-            slot = lax.rem(target + members // 2, members)
+            slot = lax.rem(target + members - 3 * members // 4, members)
             out[pl.ds(slot, 1)] = packed[place:place + 1].reshape(1, 1, LANES)
 
     if outer > NEAR:
@@ -227,11 +227,11 @@
         same = [[2 * i + core for i in range(members)] for core in range(2)]
         parts = [lax.all_gather(hidden, "vocab", axis_index_groups=same, tiled=True)]
     else:
-        line, across = [hidden], [move(hidden, 0, 1)]
-        for step in range(1, outer):
-            line.append(move(hidden, step, 0))
-            origin = (hidden, step) if step in DIRECT else (line[-1], 0)
-            across.append(move(*origin, 1))
+        line = [hidden] + [move(hidden, step, 0) for step in range(1, outer)]
+        across = [move(hidden, 0, 1)]
+        across += [move(hidden, step, 1) for step in range(1, min(outer, DIRECT + 1))]
+        if len(line) > len(across):
+            across.append(move(jnp.concatenate(line[len(across):], axis=0), 0, 1))
         parts = line + across
     other = lax.ppermute(embedding, "vocab", [(i, i ^ 1) for i in range(count)])
     state = (prev_tokens, last_stamp[None], sample_begin[None], seq_length[None], chosen)
@@ -257,7 +257,7 @@
         name="stats",
         compiler_params=pltpu.CompilerParams(vmem_limit_bytes=GRANT),
     )(*parts, table, other, limits)
-    order = [(i + members // 2) % members for i in range(members)]
+    order = [(i + 3 * members // 4) % members for i in range(members)]
     same_core = [[2 * i + core for i in order] for core in range(2)]
     got = lax.all_to_all(stats, "vocab", 0, 0, axis_index_groups=same_core, tiled=True)
     picked, stamped = pl.pallas_call(

time: 26.5 us -> 29.6 us (1.12)
  waiting for transfers between devices: 2.26 us -> 4.7 us
  blocking collectives: 8.72 us -> 9.06 us
    ppermute x7 -> x6, waiting for transfers between devices: 2.26 us -> 4.7 us  [move(): return lax.ppermute(array, 'vocab', pairs)]
    all_to_all x1, blocking collectives: 8.72 us -> 9.06 us  [per_device(): lax.all_to_all(stats, 'vocab', 0, 0, axis_index_groups=same_core, tiled=T...]
    ppermute x7 -> x6, starting transfers between devices: 10.9 us -> 11.2 us  [move(): return lax.ppermute(array, 'vocab', pairs)]
  transfers between devices with their start and end apart: 8 -> 7, of which waited for: 3 -> 4; matrix products, arithmetic and copies ran while one was open for 0% -> 0% of each run, Pallas kernels for 5% -> 5%
where the time goes in v4:
time: 29.6 us; the launch traced here: 29.4 us
  starting transfers between devices  11.7 us (40%)
  blocking collectives  9.06 us (31%)
  waiting for transfers between devices  4.7 us (16%)
  Pallas kernels  3.23 us (11%)
  between operations  0.67 us (2%)
    ppermute x6, starting transfers between devices, move(): return lax.ppermute(array, 'vocab', pairs)  11.2 us
    all_to_all x1, blocking collectives, per_device(): lax.all_to_all(stats, 'vocab', 0, 0, axis_index_groups=same_core, tiled=T...  9.06 us
    ppermute x6, waiting for transfers between devices, move(): return lax.ppermute(array, 'vocab', pairs)  4.7 us
    pallas_call x1, Pallas kernels, per_device(): pl.pallas_call(functools.partial(prep_kernel, members, row_dev, stamp_beg...  1.37 us
    pallas_call x1, Pallas kernels, per_device(): pl.pallas_call(functools.partial(stats_kernel, members, row_dev, stamp_be...  1.13 us
    pallas_call x1, Pallas kernels, per_device(): pl.pallas_call(functools.partial(final_kernel, row_dev, stamp_begin, own_...  0.73 us
  transfers between devices with their start and end apart: 7, of which 4 were waited for; matrix products, arithmetic and copies ran while one was open for 0% of the time, Pallas kernels for 5%

profile of v4, /device:TPU:0, one launch (start us, length us, event | category | flops | bytes accessed | tf_op | source)
XLA Modules:
  0.0 29.4 jit_solution(5720757844294247066)
XLA Ops:
  0.6 0.0 copy-start
  0.6 0.6 %collective-permute-start.6 = (bf16[384,1280]{1,0:T(8,128)(2,1)}, bf16[384,1280]{1,0:T(8,128)(2,1)S(1)}, u32[]{:S(2)}, u32[]{:S(2)}) collective-permute-start(bf16[384,1280]{1,0:T(8,128)(2,1)} %refs_5_.1), channel_id=1, source_target_pairs={{0,1},{1,0},{2,3},{3,2},{4,5},{5,4},{6,7},{7,6},{8,9},{9,8},{10,11... | collective-permute-start | bytes 2949128 | tf_op jit(solution)/shard_map/ppermute | solution.py:236
  1.2 2.6 %collective-permute-start.2 = (bf16[16,1280]{1,0:T(8,128)(2,1)}, bf16[16,1280]{1,0:T(8,128)(2,1)S(1)}, u32[]{:S(2)}, u32[]{:S(2)}) collective-permute-start(bf16[16,1280]{1,0:T(8,128)(2,1)} %refs_6_.1), channel_id=1, source_target_pairs={{0,4},{1,5},{2,6},{3,7},{4,8},{5,9},{6,10},{7,11},{8,12},{9,13},{1... | collective-permute-start | bytes 122888 | tf_op jit(solution)/shard_map/ppermute | solution.py:224
  3.8 2.6 %collective-permute-start.1 = (bf16[16,1280]{1,0:T(8,128)(2,1)}, bf16[16,1280]{1,0:T(8,128)(2,1)S(1)}, u32[]{:S(2)}, u32[]{:S(2)}) collective-permute-start(bf16[16,1280]{1,0:T(8,128)(2,1)} %refs_6_.1), channel_id=1, source_target_pairs={{0,8},{1,9},{2,10},{3,11},{4,12},{5,13},{6,14},{7,15},{8,0},{9,1},... | collective-permute-start | bytes 122888 | tf_op jit(solution)/shard_map/ppermute | solution.py:224
  6.4 1.9 %collective-permute-done.2.refs_3_ = bf16[16,1280]{1,0:T(8,128)(2,1)S(1)} collective-permute-done((bf16[16,1280]{1,0:T(8,128)(2,1)}, bf16[16,1280]{1,0:T(8,128)(2,1)S(1)}, u32[]{:S(2)}, u32[]{:S(2)}) %collective-permute-start.2) | collective-permute-done | bytes 40992 | tf_op jit(solution)/shard_map/ppermute | solution.py:224
  8.3 1.7 %collective-permute-done.1.refs_2_ = bf16[16,1280]{1,0:T(8,128)(2,1)S(1)} collective-permute-done((bf16[16,1280]{1,0:T(8,128)(2,1)}, bf16[16,1280]{1,0:T(8,128)(2,1)S(1)}, u32[]{:S(2)}, u32[]{:S(2)}) %collective-permute-start.1) | collective-permute-done | bytes 40992 | tf_op jit(solution)/shard_map/ppermute | solution.py:224
  10.0 1.5 %collective-permute-start.5 = (bf16[32,1280]{1,0:T(8,128)(2,1)S(1)}, bf16[32,1280]{1,0:T(8,128)(2,1)S(1)}, u32[]{:S(2)}, u32[]{:S(2)}) collective-permute-start(bf16[32,1280]{1,0:T(8,128)(2,1)S(1)} %pad_maximum_fusion), channel_id=1, source_target_pairs={{0,2},{1,3},{2,0},{3,1},{4,6},{5,7},{6,4},{7,5},{8,10},{9,11},{10,... | collective-permute-start | bytes 245768 | tf_op jit(solution)/shard_map/ppermute | solution.py:224
  11.5 0.0 copy-done
  11.5 1.2 %collective-permute-start = (bf16[16,1280]{1,0:T(8,128)(2,1)S(1)}, bf16[16,1280]{1,0:T(8,128)(2,1)S(1)}, u32[]{:S(2)}, u32[]{:S(2)}) collective-permute-start(bf16[16,1280]{1,0:T(8,128)(2,1)S(1)} %copy-done), channel_id=1, source_target_pairs={{0,12},{1,13},{2,14},{3,15},{4,0},{5,1},{6,2},{7,3},{8,4},{9,5},{1... | collective-permute-start | bytes 122888 | tf_op jit(solution)/shard_map/ppermute | solution.py:224
  12.7 1.8 %collective-permute-start.4 = (bf16[16,1280]{1,0:T(8,128)(2,1)S(1)}, bf16[16,1280]{1,0:T(8,128)(2,1)S(1)}, u32[]{:S(2)}, u32[]{:S(2)}) collective-permute-start(bf16[16,1280]{1,0:T(8,128)(2,1)S(1)} %copy-done), channel_id=1, source_target_pairs={{0,14},{1,15},{2,12},{3,13},{4,2},{5,3},{6,0},{7,1},{8,6},{9,7},{1... | collective-permute-start | bytes 122888 | tf_op jit(solution)/shard_map/ppermute | solution.py:224
  14.5 1.5 %collective-permute-start.3 = (bf16[16,1280]{1,0:T(8,128)(2,1)S(1)}, bf16[16,1280]{1,0:T(8,128)(2,1)S(1)}, u32[]{:S(2)}, u32[]{:S(2)}) collective-permute-start(bf16[16,1280]{1,0:T(8,128)(2,1)S(1)} %copy-done), channel_id=1, source_target_pairs={{0,2},{1,3},{2,0},{3,1},{4,6},{5,7},{6,4},{7,5},{8,10},{9,11},{10,... | collective-permute-start | bytes 122888 | tf_op jit(solution)/shard_map/ppermute | solution.py:224
  16.0 1.4 %prep.1 = (s32[8,128]{1,0:T(8,128)S(1)}, bf16[384,1280]{1,0:T(8,128)(2,1)S(1)}, bf16[16,1280]{1,0:T(8,128)(2,1)S(1)}) custom-call(s32[2,256]{1,0:T(2,128)} %refs_0_.1, s32[1,256]{1,0:T(1,128)} %bitcast.4, s32[1,256]{1,0:T(1,128)} %bitcast.5, s32[1,256]{1,0:T(1,128)} %bitcast.6, s32[5,256]{1,0:T(8,128)} %refs_4_.1, bf16[384,1280]{1,0:T(8,128)(2,1)} %refs_5_.1, ...), custom_call_target="tpu_custom_call" | custom-call | tf_op jit(solution)/shard_map/prep/pallas_call | solution.py:238
  17.3 0.0 collective-permute-done.refs_1_
  17.3 0.3 collective-permute-done.4.refs_5_
  17.6 0.9 %collective-permute-done.3.refs_4_ = bf16[16,1280]{1,0:T(8,128)(2,1)S(1)} collective-permute-done((bf16[16,1280]{1,0:T(8,128)(2,1)S(1)}, bf16[16,1280]{1,0:T(8,128)(2,1)S(1)}, u32[]{:S(2)}, u32[]{:S(2)}) %collective-permute-start.3) | collective-permute-done | bytes 40992 | tf_op jit(solution)/shard_map/ppermute | solution.py:224
  18.5 0.0 collective-permute-done.5.refs_6_
  18.5 0.0 collective-permute-done.6.refs_8_
  18.5 1.1 %stats.1 = f32[8,1,128]{2,1,0:T(1,128)S(1)} custom-call(bf16[16,1280]{1,0:T(8,128)(2,1)S(1)} %get-tuple-element.7.refs_0_, bf16[16,1280]{1,0:T(8,128)(2,1)S(1)} %collective-permute-done.refs_1_, bf16[16,1280]{1,0:T(8,128)(2,1)S(1)} %collective-permute-done.1.refs_2_, bf16[16,1280]{1,0:T(8,128)(2,1)S(1)} %collective-permute-done.2.refs_3_, ...), custom_call_target="tpu_custom_call" | custom-call | tf_op jit(solution)/shard_map/stats/pallas_call | solution.py:254
  19.6 9.1 %all_to_all.5.got = f32[8,1,128]{2,1,0:T(1,128)S(1)} all-to-all(f32[8,1,128]{2,1,0:T(1,128)S(1)} %stats.1), channel_id=1, replica_groups={{12,14,0,2,4,6,8,10},{13,15,1,3,5,7,9,11},{28,30,16,18,20,22,24,26},{29..., dimensions={0} | all-to-all | bytes 8192 | tf_op jit(solution)/shard_map/all_to_all | solution.py:262
  28.7 0.7 %final.1 = (f32[5,16]{1,0:T(8,128)}, f32[1,16]{1,0:T(1,128)}) custom-call(f32[8,1,128]{2,1,0:T(1,128)S(1)} %all_to_all.5.got, s32[8,128]{1,0:T(8,128)S(1)} %get-tuple-element.9.refs_9_.limits), custom_call_target="tpu_custom_call" | custom-call | tf_op jit(solution)/shard_map/final/pallas_call | solution.py:263
  (1 shorter events, 0.0 us)
Async XLA Ops:
  0.6 10.9 %copy-start = (bf16[16,1280]{1,0:T(8,128)(2,1)S(1)}, bf16[16,1280]{1,0:T(8,128)(2,1)}, u32[]{:S(2)}) copy-start(bf16[16,1280]{1,0:T(8,128)(2,1)} %refs_6_.1) | copy-start | bytes 122884
  0.6 17.8 %collective-permute-start.6 = (bf16[384,1280]{1,0:T(8,128)(2,1)}, bf16[384,1280]{1,0:T(8,128)(2,1)S(1)}, u32[]{:S(2)}, u32[]{:S(2)}) collective-permute-start(bf16[384,1280]{1,0:T(8,128)(2,1)} %refs_5_.1), channel_id=1, source_target_pairs={{0,1},{1,0},{2,3},{3,2},{4,5},{5,4},{6,7},{7,6},{8,9},{9,8},{10,11... | collective-permute-start | bytes 2949128 | tf_op jit(solution)/shard_map/ppermute | solution.py:236
  1.2 7.1 %collective-permute-start.2 = (bf16[16,1280]{1,0:T(8,128)(2,1)}, bf16[16,1280]{1,0:T(8,128)(2,1)S(1)}, u32[]{:S(2)}, u32[]{:S(2)}) collective-permute-start(bf16[16,1280]{1,0:T(8,128)(2,1)} %refs_6_.1), channel_id=1, source_target_pairs={{0,4},{1,5},{2,6},{3,7},{4,8},{5,9},{6,10},{7,11},{8,12},{9,13},{1... | collective-permute-start | bytes 122888 | tf_op jit(solution)/shard_map/ppermute | solution.py:224
  3.8 6.2 %collective-permute-start.1 = (bf16[16,1280]{1,0:T(8,128)(2,1)}, bf16[16,1280]{1,0:T(8,128)(2,1)S(1)}, u32[]{:S(2)}, u32[]{:S(2)}) collective-permute-start(bf16[16,1280]{1,0:T(8,128)(2,1)} %refs_6_.1), channel_id=1, source_target_pairs={{0,8},{1,9},{2,10},{3,11},{4,12},{5,13},{6,14},{7,15},{8,0},{9,1},... | collective-permute-start | bytes 122888 | tf_op jit(solution)/shard_map/ppermute | solution.py:224
  10.0 8.5 %collective-permute-start.5 = (bf16[32,1280]{1,0:T(8,128)(2,1)S(1)}, bf16[32,1280]{1,0:T(8,128)(2,1)S(1)}, u32[]{:S(2)}, u32[]{:S(2)}) collective-permute-start(bf16[32,1280]{1,0:T(8,128)(2,1)S(1)} %pad_maximum_fusion), channel_id=1, source_target_pairs={{0,2},{1,3},{2,0},{3,1},{4,6},{5,7},{6,4},{7,5},{8,10},{9,11},{10,... | collective-permute-start | bytes 245768 | tf_op jit(solution)/shard_map/ppermute | solution.py:224
  11.5 5.8 %collective-permute-start = (bf16[16,1280]{1,0:T(8,128)(2,1)S(1)}, bf16[16,1280]{1,0:T(8,128)(2,1)S(1)}, u32[]{:S(2)}, u32[]{:S(2)}) collective-permute-start(bf16[16,1280]{1,0:T(8,128)(2,1)S(1)} %copy-done), channel_id=1, source_target_pairs={{0,12},{1,13},{2,14},{3,15},{4,0},{5,1},{6,2},{7,3},{8,4},{9,5},{1... | collective-permute-start | bytes 122888 | tf_op jit(solution)/shard_map/ppermute | solution.py:224
  12.7 4.9 %collective-permute-start.4 = (bf16[16,1280]{1,0:T(8,128)(2,1)S(1)}, bf16[16,1280]{1,0:T(8,128)(2,1)S(1)}, u32[]{:S(2)}, u32[]{:S(2)}) collective-permute-start(bf16[16,1280]{1,0:T(8,128)(2,1)S(1)} %copy-done), channel_id=1, source_target_pairs={{0,14},{1,15},{2,12},{3,13},{4,2},{5,3},{6,0},{7,1},{8,6},{9,7},{1... | collective-permute-start | bytes 122888 | tf_op jit(solution)/shard_map/ppermute | solution.py:224
  14.5 4.0 %collective-permute-start.3 = (bf16[16,1280]{1,0:T(8,128)(2,1)S(1)}, bf16[16,1280]{1,0:T(8,128)(2,1)S(1)}, u32[]{:S(2)}, u32[]{:S(2)}) collective-permute-start(bf16[16,1280]{1,0:T(8,128)(2,1)S(1)} %copy-done), channel_id=1, source_target_pairs={{0,2},{1,3},{2,0},{3,1},{4,6},{5,7},{6,4},{7,5},{8,10},{9,11},{10,... | collective-permute-start | bytes 122888 | tf_op jit(solution)/shard_map/ppermute | solution.py:224
